TPU v7x, 64 devices: a 2x2x8 block of a 4x4x8 slice. The times are simulated.
64 devices in a mesh: dp: 4 (over x, y), cp: 16 (over z, core).
Axes of the slice: x: 2, y: 2, z: 8, core: 2. Of those that a mesh axis runs over, the one named last changes fastest.
The devices are a block of a 4x4x8 slice.
Arguments:
- latents: bfloat16 [8, 128, 128, 4], P('dp', 'cp'), parts along dimension 0
- w_in: bfloat16 [3, 3, 4, 512], replicated
- b_in: bfloat16 [512], replicated
- w_conv: bfloat16 [4, 3, 3, 512, 512], replicated
- b_conv: bfloat16 [4, 512], replicated
- gn_scale: bfloat16 [5, 512], replicated
- gn_shift: bfloat16 [5, 512], replicated
- w_attn: bfloat16 [4, 512, 512], replicated
- b_attn: bfloat16 [4, 512], replicated
Outputs:
- output: bfloat16 [8, 128, 128, 512], P('dp', 'cp'), parts along dimension 0
There are 4 independent parts. A program takes and returns all parts, laid end to end along the dimension named above; an argument that names none is the same for every part.
All inputs are finite; a program needn't handle non-finite values.
Results may differ from a plain program's by a relative error of at most 0.02.
Values are sent between devices in bfloat16 or wider.
A program may use at most 768 MiB of HBM per device.

v0:
```python
import jax
import jax.numpy as jnp
from jax import lax
from jax.sharding import PartitionSpec as P

GROUPS = 32
GN_EPS = 1e-6
QUERY_TOKENS = 512


def group_norm(x_val, norm_gain, norm_bias, n_dev):
    n_batch, n_rows, n_width, n_chan = x_val.shape
    grouped = x_val.reshape(n_batch, n_rows, n_width, GROUPS, n_chan // GROUPS)
    local_sums = jnp.stack([jnp.sum(grouped, axis=(1, 2, 4), dtype=jnp.float32), jnp.sum(jnp.square(grouped.astype(jnp.float32)), axis=(1, 2, 4))])
    totals = lax.psum(local_sums, 'cp')
    elem_count = n_rows * n_width * (n_chan // GROUPS) * n_dev
    grp_mean = totals[0] / elem_count
    inv_std = lax.rsqrt(totals[1] / elem_count - jnp.square(grp_mean) + GN_EPS)
    normed = (grouped - grp_mean[:, None, None, :, None]) * inv_std[:, None, None, :, None]
    return normed.reshape(x_val.shape) * norm_gain + norm_bias


def conv_rows(x_val, weight, conv_bias, n_dev):
    down_pairs = [(sender, sender + 1) for sender in range(n_dev - 1)]
    up_pairs = [(sender + 1, sender) for sender in range(n_dev - 1)]
    from_above = lax.ppermute(x_val[:, -1:], 'cp', down_pairs)
    from_below = lax.ppermute(x_val[:, :1], 'cp', up_pairs)
    padded = jnp.concatenate([from_above, x_val, from_below], axis=1)
    conv_out = lax.conv_general_dilated(padded, weight, (1, 1), ((0, 0), (1, 1)), dimension_numbers=('NHWC', 'HWIO', 'NHWC'), preferred_element_type=jnp.float32)
    return conv_out + conv_bias


def resnet_block(h_val, w_conv, b_conv, gn_scale, gn_shift, conv_idx, norm_idx, n_dev):
    act_in = jax.nn.silu(group_norm(h_val, gn_scale[norm_idx], gn_shift[norm_idx], n_dev)).astype(jnp.bfloat16)
    mid_act = conv_rows(act_in, w_conv[conv_idx], b_conv[conv_idx], n_dev).astype(jnp.bfloat16)
    act_two = jax.nn.silu(group_norm(mid_act, gn_scale[norm_idx + 1], gn_shift[norm_idx + 1], n_dev)).astype(jnp.bfloat16)
    conv_two = conv_rows(act_two, w_conv[conv_idx + 1], b_conv[conv_idx + 1], n_dev)
    return (h_val + conv_two).astype(jnp.bfloat16)


def attend(queries, keys_all, vals_all):
    n_batch, n_query, n_chan = queries.shape
    block_len = max([divisor for divisor in range(1, min(n_query, QUERY_TOKENS) + 1) if n_query % divisor == 0])
    n_blocks = n_query // block_len
    q_blocks = queries.reshape(n_batch * n_blocks, block_len, n_chan)
    att_scale = n_chan ** -0.5

    def attend_step(step_idx, out_buf):
        q_block = lax.dynamic_index_in_dim(q_blocks, step_idx, 0, keepdims=False)
        sample_idx = step_idx // n_blocks
        k_sample = lax.dynamic_index_in_dim(keys_all, sample_idx, 0, keepdims=False)
        v_sample = lax.dynamic_index_in_dim(vals_all, sample_idx, 0, keepdims=False)
        scores = lax.dot_general(q_block, k_sample, (((1,), (1,)), ((), ())), preferred_element_type=jnp.float32) * att_scale
        attn_prob = jax.nn.softmax(scores, axis=-1).astype(jnp.bfloat16)
        o_block = jnp.dot(attn_prob, v_sample, preferred_element_type=jnp.float32).astype(jnp.bfloat16)
        return lax.dynamic_update_index_in_dim(out_buf, o_block, step_idx, 0)

    attended = lax.fori_loop(0, n_batch * n_blocks, attend_step, jnp.zeros_like(q_blocks))
    return attended.reshape(n_batch, n_query, n_chan)


def solution(mesh):
    n_dev = mesh.shape['cp']

    def local_fn(latents, w_in, b_in, w_conv, b_conv, gn_scale, gn_shift, w_attn, b_attn):
        hidden = conv_rows(latents, w_in, b_in, n_dev).astype(jnp.bfloat16)
        hidden = resnet_block(hidden, w_conv, b_conv, gn_scale, gn_shift, 0, 0, n_dev)
        n_batch, n_rows, n_width, n_chan = hidden.shape
        normed = group_norm(hidden, gn_scale[2], gn_shift[2], n_dev).astype(jnp.bfloat16).reshape(-1, n_chan)

        def project(j_idx):
            proj = jnp.dot(normed, w_attn[j_idx], preferred_element_type=jnp.float32) + b_attn[j_idx]
            return proj.astype(jnp.bfloat16).reshape(n_batch, n_rows * n_width, n_chan)

        keys_all = lax.all_gather(project(1), 'cp', axis=1, tiled=True)
        vals_all = lax.all_gather(project(2), 'cp', axis=1, tiled=True)
        attended = attend(project(0), keys_all, vals_all).reshape(-1, n_chan)
        proj_out = jnp.dot(attended, w_attn[3], preferred_element_type=jnp.float32) + b_attn[3]
        hidden = (hidden + proj_out.reshape(hidden.shape)).astype(jnp.bfloat16)
        return resnet_block(hidden, w_conv, b_conv, gn_scale, gn_shift, 2, 3, n_dev)

    band_spec = P('dp', 'cp')
    whole_spec = P()
    return jax.shard_map(local_fn, mesh=mesh, in_specs=(band_spec,) + (whole_spec,) * 8, out_specs=band_spec, check_vma=False)
```

profile of v0, /device:TPU:21, one launch (start us, length us, event | category | flops | bytes accessed | tf_op | source)
XLA Modules:
  0.0 970.2 jit_solution(9209154838814471915)
XLA Ops:
  7.3 5.1 collective-permute-start
  12.4 2.8 collective-permute-start.1
  23.3 4.1 convert_multiply_fusion.1
  29.0 4.8 copy.60
  34.4 26.7 %psum.35 = f32[2,2,32]{2,1,0:T(2,128)S(1)} all-reduce(f32[2,2,32]{2,1,0:T(2,128)S(1)} %pad_maximum_fusion), channel_id=1, replica_groups=mesh['dp'=4,'cp'=16] {'cp'}, use_global_device_ids=true, to_apply=%region_4.5 | all-reduce | flops 128 | bytes 1024 | tf_op jit(solution)/shard_map/psum | solution.py:15
  62.6 5.2 multiply_convert_fusion.2
  67.8 2.6 copy.64
  72.0 3.8 collective-permute-start.3
  82.5 3.0 maximum_bitcast_fusion
  85.5 2.7 copy.104
  88.2 2.3 pad.2.clone
  90.7 2.9 fusion.59
  93.6 15.0 %convert_multiply_fusion.4 = (f32[8,16,17,512]{3,1,2,0:T(8,128)}, bf16[8,16,17,512]{3,1,2,0:T(8,128)(2,1)S(1)}) fusion(f32[512]{0:T(512)S(1)} %bitcast.328, bf16[4,3,3,512,512]{4,3,2,1,0:T(8,128)(2,1)} %param.14, bf16[10,2,8,19,512]{4,1,3,2,0:T(2,128)(2,1)S(1)} %fusion.59, pred[16,17]{0,1:T(8,128)(4,1)S(1)} %copy-done.17), kind=kOutput, calls=%fused_computation.110 | convolution fusion | flops 10273226752 | bytes 14518544 | tf_op jit(solution)/shard_map/conv_general_dilated | solution.py:29
  111.8 4.9 copy.71
  117.1 22.1 %psum.36 = f32[2,2,32]{2,1,0:T(2,128)S(1)} all-reduce(f32[2,2,32]{2,1,0:T(2,128)S(1)} %pad_maximum_fusion.1), channel_id=1, replica_groups=mesh['dp'=4,'cp'=16] {'cp'}, use_global_device_ids=true, to_apply=%region_9.10 | all-reduce | flops 128 | bytes 1024 | tf_op jit(solution)/shard_map/psum | solution.py:15
  141.2 5.2 multiply_convert_fusion.1
  146.3 2.6 copy.75
  150.5 4.4 collective-permute-start.5
  161.1 3.1 maximum_bitcast_fusion.1
  164.2 2.7 copy.105
  166.9 2.3 pad.4.clone
  169.4 2.9 fusion.60
  172.3 15.3 %convert_multiply_fusion.3 = (f32[8,16,17,512]{3,1,2,0:T(8,128)}, bf16[8,16,17,512]{3,1,2,0:T(8,128)(2,1)S(1)}) fusion(f32[512]{0:T(512)S(1)} %bitcast.327, bf16[4,3,3,512,512]{4,3,2,1,0:T(8,128)(2,1)} %param.14, bf16[10,2,8,19,512]{4,1,3,2,0:T(2,128)(2,1)S(1)} %fusion.60, pred[16,17]{0,1:T(8,128)(4,1)S(1)} %copy-done.17, ...), kind=kOutput, calls=%fused_computation.109 | convolution fusion | flops 10275454976 | bytes 16746768 | tf_op jit(solution)/shard_map/conv_general_dilated | solution.py:29
  192.7 4.9 copy.82
  198.1 23.2 %psum.37 = f32[2,2,32]{2,1,0:T(2,128)S(1)} all-reduce(f32[2,2,32]{2,1,0:T(2,128)S(1)} %pad_maximum_fusion.2), channel_id=1, replica_groups=mesh['dp'=4,'cp'=16] {'cp'}, use_global_device_ids=true, to_apply=%region_14.15 | all-reduce | flops 128 | bytes 1024 | tf_op jit(solution)/shard_map/psum | solution.py:15
  223.2 5.4 fusion.41
  230.6 3.7 add_convert_fusion.5
  234.4 3.7 add_convert_fusion.4
  238.2 3.6 add_convert_fusion.6
  241.8 170.0 %all-gather.3.cloned.1.call-done = bf16[2,16384,512]{2,1,0:T(8,128)(2,1)} async-done(((bf16[2,1024,512]{2,1,0:T(8,128)(2,1)}), bf16[2,16384,512]{2,1,0:T(8,128)(2,1)}) %all-gather.3.cloned.1.call-update) | async-done | bytes 33554448 | tf_op jit(solution)/shard_map/all_gather | solution.py:75
  411.8 171.2 %all-gather.5.cloned.1.call-done = bf16[2,16384,512]{2,1,0:T(8,128)(2,1)} async-done(((bf16[2,1024,512]{2,1,0:T(8,128)(2,1)}), bf16[2,16384,512]{2,1,0:T(8,128)(2,1)}) %all-gather.5.cloned.1.call-update) | async-done | bytes 33554448 | tf_op jit(solution)/shard_map/all_gather | solution.py:76
  583.1 221.8 %while.15 = (s32[]{:T(128)}, bf16[4,512,512]{2,1,0:T(8,128)(2,1)}, bf16[4,512,512]{2,1,0:T(8,128)(2,1)}, bf16[2,16384,512]{2,1,0:T(8,128)(2,1)}, bf16[2,16384,51...) while((s32[]{:T(128)}, bf16[4,512,512]{2,1,0:T(8,128)(2,1)}, ...), condition=%wide.region_18.19_spmd, body=%wide.region_15.18_spmd.sunk | while | flops 17255628800 | bytes 135277776 | solution.py:58
  583.3 19.9 %multiply_reduce_fusion.2 = (f32[512]{0:T(512)S(1)}, f32[512,16384]{1,0:T(8,128)}) fusion(bf16[2,16384,512]{2,1,0:T(8,128)(2,1)} %get-tuple-element.246, s32[]{:T(128)S(6)} %select_n.38, bf16[4,512,512]{2,1,0:T(8,128)(2,1)} %get-tuple-element.245, s32[]{:T(128)} %get-tuple-element.234), kind=kOutput, calls=%fused_computation.2.clone.1 | convolution fusion | flops 8606711808 | bytes 50858500 | tf_op jit(solution)/shard_map/while/body/eval_jaxpr/dot_general | solution.py:53
  603.2 14.1 %fusion.139 = f32[512]{0:T(512)S(1)} fusion(f32[512,16384]{1,0:T(8,128)} %get-tuple-element.223, f32[512]{0:T(512)S(1)} %get-tuple-element.224), kind=kLoop, calls=%fused_computation.3.clone.1 | loop fusion | flops 25165312 | bytes 33558528 | tf_op jit(solution)/shard_map/while/body/eval_jaxpr/reduce_sum | solution.py:54
  617.2 21.4 %fusion.140 = bf16[4,512,512]{2,1,0:T(8,128)(2,1)} fusion(bf16[4,512,512]{2,1,0:T(8,128)(2,1)} %get-tuple-element.235, s32[]{:T(128)} %get-tuple-element.234, bf16[2,16384,512]{2,1,0:T(8,128)(2,1)} %get-tuple-element.247, s32[]{:T(128)S(6)} %select_n.38, f32[512,16384]{1,0:T(8,128)} %get-tuple-element.223, f32[512]{0:T(512)S(1)} %fusion.139, ...), kind=kOutput, calls=%fused_computation.12.clone.1 | convolution fusion | flops 8623751168 | bytes 50860548 | tf_op jit(solution)/shard_map/while/body/eval_jaxpr/dot_general | solution.py:55
  638.7 19.9 %multiply_reduce_fusion.2 = (f32[512]{0:T(512)S(1)}, f32[512,16384]{1,0:T(8,128)}) fusion(bf16[2,16384,512]{2,1,0:T(8,128)(2,1)} %get-tuple-element.246, s32[]{:T(128)S(6)} %select_n.38, bf16[4,512,512]{2,1,0:T(8,128)(2,1)} %get-tuple-element.245, s32[]{:T(128)} %get-tuple-element.234), kind=kOutput, calls=%fused_computation.2.clone.1 | convolution fusion | flops 8606711808 | bytes 50858500 | tf_op jit(solution)/shard_map/while/body/eval_jaxpr/dot_general | solution.py:53
  658.6 14.1 %fusion.139 = f32[512]{0:T(512)S(1)} fusion(f32[512,16384]{1,0:T(8,128)} %get-tuple-element.223, f32[512]{0:T(512)S(1)} %get-tuple-element.224), kind=kLoop, calls=%fused_computation.3.clone.1 | loop fusion | flops 25165312 | bytes 33558528 | tf_op jit(solution)/shard_map/while/body/eval_jaxpr/reduce_sum | solution.py:54
  672.6 21.4 %fusion.140 = bf16[4,512,512]{2,1,0:T(8,128)(2,1)} fusion(bf16[4,512,512]{2,1,0:T(8,128)(2,1)} %get-tuple-element.235, s32[]{:T(128)} %get-tuple-element.234, bf16[2,16384,512]{2,1,0:T(8,128)(2,1)} %get-tuple-element.247, s32[]{:T(128)S(6)} %select_n.38, f32[512,16384]{1,0:T(8,128)} %get-tuple-element.223, f32[512]{0:T(512)S(1)} %fusion.139, ...), kind=kOutput, calls=%fused_computation.12.clone.1 | convolution fusion | flops 8623751168 | bytes 50860548 | tf_op jit(solution)/shard_map/while/body/eval_jaxpr/dot_general | solution.py:55
  694.1 19.9 %multiply_reduce_fusion.2 = (f32[512]{0:T(512)S(1)}, f32[512,16384]{1,0:T(8,128)}) fusion(bf16[2,16384,512]{2,1,0:T(8,128)(2,1)} %get-tuple-element.246, s32[]{:T(128)S(6)} %select_n.38, bf16[4,512,512]{2,1,0:T(8,128)(2,1)} %get-tuple-element.245, s32[]{:T(128)} %get-tuple-element.234), kind=kOutput, calls=%fused_computation.2.clone.1 | convolution fusion | flops 8606711808 | bytes 50858500 | tf_op jit(solution)/shard_map/while/body/eval_jaxpr/dot_general | solution.py:53
  714.0 14.1 %fusion.139 = f32[512]{0:T(512)S(1)} fusion(f32[512,16384]{1,0:T(8,128)} %get-tuple-element.223, f32[512]{0:T(512)S(1)} %get-tuple-element.224), kind=kLoop, calls=%fused_computation.3.clone.1 | loop fusion | flops 25165312 | bytes 33558528 | tf_op jit(solution)/shard_map/while/body/eval_jaxpr/reduce_sum | solution.py:54
  728.0 21.4 %fusion.140 = bf16[4,512,512]{2,1,0:T(8,128)(2,1)} fusion(bf16[4,512,512]{2,1,0:T(8,128)(2,1)} %get-tuple-element.235, s32[]{:T(128)} %get-tuple-element.234, bf16[2,16384,512]{2,1,0:T(8,128)(2,1)} %get-tuple-element.247, s32[]{:T(128)S(6)} %select_n.38, f32[512,16384]{1,0:T(8,128)} %get-tuple-element.223, f32[512]{0:T(512)S(1)} %fusion.139, ...), kind=kOutput, calls=%fused_computation.12.clone.1 | convolution fusion | flops 8623751168 | bytes 50860548 | tf_op jit(solution)/shard_map/while/body/eval_jaxpr/dot_general | solution.py:55
  749.5 19.9 %multiply_reduce_fusion.2 = (f32[512]{0:T(512)S(1)}, f32[512,16384]{1,0:T(8,128)}) fusion(bf16[2,16384,512]{2,1,0:T(8,128)(2,1)} %get-tuple-element.246, s32[]{:T(128)S(6)} %select_n.38, bf16[4,512,512]{2,1,0:T(8,128)(2,1)} %get-tuple-element.245, s32[]{:T(128)} %get-tuple-element.234), kind=kOutput, calls=%fused_computation.2.clone.1 | convolution fusion | flops 8606711808 | bytes 50858500 | tf_op jit(solution)/shard_map/while/body/eval_jaxpr/dot_general | solution.py:53
  769.3 14.1 %fusion.139 = f32[512]{0:T(512)S(1)} fusion(f32[512,16384]{1,0:T(8,128)} %get-tuple-element.223, f32[512]{0:T(512)S(1)} %get-tuple-element.224), kind=kLoop, calls=%fused_computation.3.clone.1 | loop fusion | flops 25165312 | bytes 33558528 | tf_op jit(solution)/shard_map/while/body/eval_jaxpr/reduce_sum | solution.py:54
  783.4 21.4 %fusion.140 = bf16[4,512,512]{2,1,0:T(8,128)(2,1)} fusion(bf16[4,512,512]{2,1,0:T(8,128)(2,1)} %get-tuple-element.235, s32[]{:T(128)} %get-tuple-element.234, bf16[2,16384,512]{2,1,0:T(8,128)(2,1)} %get-tuple-element.247, s32[]{:T(128)S(6)} %select_n.38, f32[512,16384]{1,0:T(8,128)} %get-tuple-element.223, f32[512]{0:T(512)S(1)} %fusion.139, ...), kind=kOutput, calls=%fused_computation.12.clone.1 | convolution fusion | flops 8623751168 | bytes 50860548 | tf_op jit(solution)/shard_map/while/body/eval_jaxpr/dot_general | solution.py:55
  804.9 3.1 convolution_add_fusion
  808.0 3.1 convert_reduce_fusion
  811.5 23.4 %psum.38 = f32[2,2,32]{2,1,0:T(2,128)S(1)} all-reduce(f32[2,2,32]{2,1,0:T(2,128)S(1)} %pad_maximum_fusion.3), channel_id=1, replica_groups=mesh['dp'=4,'cp'=16] {'cp'}, use_global_device_ids=true, to_apply=%region_23.24 | all-reduce | flops 128 | bytes 1024 | tf_op jit(solution)/shard_map/psum | solution.py:15
  839.5 3.2 collective-permute-start.7
  842.6 2.9 collective-permute-done.6
  845.5 4.4 collective-permute-done.7
  850.0 3.0 maximum_bitcast_fusion.2
  853.0 2.7 copy.106
  858.2 2.9 fusion.61
  861.1 15.2 %convert_multiply_fusion.2 = (f32[8,16,17,512]{3,1,2,0:T(8,128)}, bf16[8,16,17,512]{3,1,2,0:T(8,128)(2,1)S(1)}) fusion(f32[512]{0:T(512)S(1)} %bitcast.322, bf16[4,3,3,512,512]{4,3,2,1,0:T(8,128)(2,1)} %param.14, bf16[10,2,8,19,512]{4,1,3,2,0:T(2,128)(2,1)S(1)} %fusion.61, pred[16,17]{0,1:T(8,128)(4,1)S(1)} %copy-done.18), kind=kOutput, calls=%fused_computation.108 | convolution fusion | flops 10273226752 | bytes 14518544 | tf_op jit(solution)/shard_map/conv_general_dilated | solution.py:29
  879.4 4.9 copy.91
  884.7 21.4 %psum.39 = f32[2,2,32]{2,1,0:T(2,128)S(1)} all-reduce(f32[2,2,32]{2,1,0:T(2,128)S(1)} %pad_maximum_fusion.4), channel_id=1, replica_groups=mesh['dp'=4,'cp'=16] {'cp'}, use_global_device_ids=true, to_apply=%region_28.29 | all-reduce | flops 128 | bytes 1024 | tf_op jit(solution)/shard_map/psum | solution.py:15
  908.2 5.2 multiply_convert_fusion
  913.3 2.6 copy.95
  917.5 4.8 collective-permute-start.9
  928.6 3.2 maximum_bitcast_fusion.3
  931.8 2.7 copy.107
  937.0 2.9 fusion.62
  939.9 17.6 %select_add_fusion = f32[8,16,17,512]{3,1,2,0:T(8,128)S(1)} fusion(bf16[4,3,3,512,512]{4,3,2,1,0:T(8,128)(2,1)} %param.14, bf16[10,2,8,19,512]{4,1,3,2,0:T(2,128)(2,1)S(1)} %fusion.62, f32[512]{0:T(512)S(1)} %bitcast.321, pred[16,17]{0,1:T(8,128)(4,1)S(1)} %copy-done.18), kind=kOutput, calls=%fused_computation.56 | convolution fusion | flops 10269884416 | bytes 12290320 | tf_op jit(solution)/shard_map/conv_general_dilated | solution.py:29
  957.6 2.6 copy.101
  (186 shorter events, 70.0 us)
Async XLA Ops:
  6.5 16.7 %copy-start = (bf16[3,3,4,512]{3,2,1,0:T(4,128)(2,1)S(1)}, bf16[3,3,4,512]{3,2,1,0:T(4,128)(2,1)}, u32[]{:S(2)}) copy-start(bf16[3,3,4,512]{3,2,1,0:T(4,128)(2,1)} %param.12) | copy-start | bytes 110596
  6.6 405.3 %all-gather.3.cloned.1.call-start = ((), (), s32[]{:S(2)}) async-start(), calls=%async_computation | async-start | bytes 35651584 | tf_op jit(solution)/shard_map/all_gather | solution.py:75
  7.3 14.4 %collective-permute-start = (bf16[2,1,128,4]{2,3,1,0:T(4,128)(2,1)S(1)}, bf16[2,1,128,4]{2,3,1,0:T(4,128)(2,1)S(1)}, u32[]{:S(2)}, u32[]{:S(2)}) collective-permute-start(bf16[2,1,128,4]{2,3,1,0:T(4,128)(2,1)S(1)} %get-tuple-element.162), channel_id=1, source_target_pairs={{0,1},{1,2},{2,3},{3,4},{4,5},{5,6},{6,7},{7,8},{8,9},{9,10},{10,1... | collective-permute-start | bytes 6152 | tf_op jit(solution)/shard_map/ppermute | solution.py:26
  12.4 9.3 collective-permute-start.1
  72.0 10.5 %collective-permute-start.3 = (bf16[2,1,128,512]{3,1,2,0:T(2,128)(2,1)}, bf16[2,1,128,512]{3,1,2,0:T(2,128)(2,1)S(1)}, u32[]{:S(2)}, u32[]{:S(2)}) collective-permute-start(bf16[2,1,128,512]{3,1,2,0:T(2,128)(2,1)} %copy.66), channel_id=1, source_target_pairs={{1,0},{2,1},{3,2},{4,3},{5,4},{6,5},{7,6},{8,7},{9,8},{10,9},{11,1... | collective-permute-start | bytes 786440 | tf_op jit(solution)/shard_map/ppermute | solution.py:27
  76.1 5.2 collective-permute-start.2
  90.5 3.1 copy-start.17
  108.6 1.4 copy-start.6
  139.5 1.6 copy-start.7
  150.5 10.5 %collective-permute-start.5 = (bf16[2,1,128,512]{3,1,2,0:T(2,128)(2,1)}, bf16[2,1,128,512]{3,1,2,0:T(2,128)(2,1)S(1)}, u32[]{:S(2)}, u32[]{:S(2)}) collective-permute-start(bf16[2,1,128,512]{3,1,2,0:T(2,128)(2,1)} %copy.77), channel_id=1, source_target_pairs={{1,0},{2,1},{3,2},{4,3},{5,4},{6,5},{7,6},{8,7},{9,8},{10,9},{11,1... | collective-permute-start | bytes 786440 | tf_op jit(solution)/shard_map/ppermute | solution.py:27
  155.2 5.2 collective-permute-start.4
  187.6 1.4 copy-start.8
  190.3 2.0 copy-start.2
  221.6 1.6 copy-start.9
  234.4 348.7 %all-gather.5.cloned.1.call-start = ((), (), s32[]{:S(2)}) async-start(), calls=%async_computation.1 | async-start | bytes 35651584 | tf_op jit(solution)/shard_map/all_gather | solution.py:76
  583.1 221.8 %copy-start.16 = (f32[1,512]{1,0:T(1,128)S(1)}, f32[1,512]{1,0:T(1,128)}, u32[]{:S(2)}) copy-start(f32[1,512]{1,0:T(1,128)} %get-tuple-element.178) | copy-start | bytes 6148
  804.9 3.1 copy-start.3
  808.0 27.3 %copy-start.10 = (f32[1,512]{1,0:T(1,128)S(1)}, f32[1,512]{1,0:T(1,128)}, u32[]{:S(2)}) copy-start(f32[1,512]{1,0:T(1,128)} %get-tuple-element.168) | copy-start | bytes 6148
  808.0 27.3 %copy-start.11 = (f32[1,512]{1,0:T(1,128)S(1)}, f32[1,512]{1,0:T(1,128)}, u32[]{:S(2)}) copy-start(f32[1,512]{1,0:T(1,128)} %get-tuple-element.173) | copy-start | bytes 6148
  837.4 8.1 collective-permute-start.6
  839.5 10.5 %collective-permute-start.7 = (bf16[2,1,128,512]{3,1,2,0:T(2,128)(2,1)S(1)}, bf16[2,1,128,512]{3,1,2,0:T(2,128)(2,1)S(1)}, u32[]{:S(2)}, u32[]{:S(2)}) collective-permute-start(bf16[2,1,128,512]{3,1,2,0:T(2,128)(2,1)S(1)} %get-tuple-element.161), channel_id=1, source_target_pairs={{1,0},{2,1},{3,2},{4,3},{5,4},{6,5},{7,6},{8,7},{9,8},{10,9},{11,1... | collective-permute-start | bytes 786440 | tf_op jit(solution)/shard_map/ppermute | solution.py:27
  858.0 3.1 copy-start.15
  858.0 3.1 copy-start.18
  876.3 1.4 copy-start.4
  906.5 1.6 copy-start.5
  906.5 1.6 copy-start.12
  906.5 1.6 copy-start.13
  917.5 11.1 %collective-permute-start.9 = (bf16[2,1,128,512]{3,1,2,0:T(2,128)(2,1)}, bf16[2,1,128,512]{3,1,2,0:T(2,128)(2,1)S(1)}, u32[]{:S(2)}, u32[]{:S(2)}) collective-permute-start(bf16[2,1,128,512]{3,1,2,0:T(2,128)(2,1)} %copy.97), channel_id=1, source_target_pairs={{1,0},{2,1},{3,2},{4,3},{5,4},{6,5},{7,6},{8,7},{9,8},{10,9},{11,1... | collective-permute-start | bytes 786440 | tf_op jit(solution)/shard_map/ppermute | solution.py:27
  922.6 5.2 collective-permute-start.8
  936.8 3.1 copy-start.14
  960.1 2.9 copy-start.1
Sparse Core Ops, SparseCore 0:
  234.5 177.3 all-gather.2
  413.5 169.5 all-gather.4
where the time goes:
time: 982 us; the launch traced here: 970 us
  waiting for transfers between devices  354 us (36%)
  matrix products  247 us (25%)
  other arithmetic  117 us (12%)
  blocking collectives  117 us (12%)
  local copies, waits for them, and re-layouts  88.6 us (9%)
  starting transfers between devices  32.2 us (3%)
  between operations  14.6 us (1%)
    all_gather x1, waiting for transfers between devices, local_fn(): vals_all = lax.all_gather(project(2), 'cp', axis=1, tiled=True)  171 us
    all_gather x1, waiting for transfers between devices, local_fn(): keys_all = lax.all_gather(project(1), 'cp', axis=1, tiled=True)  170 us
    psum x5, blocking collectives, group_norm(): totals = lax.psum(local_sums, 'cp')  117 us
    dot_general x4, matrix products, attend_step(): jnp.dot(attn_prob, v_sample, preferred_element_type=jnp.float32)  85.8 us
    dot_general x4, matrix products, attend_step(): lax.dot_general(q_block, k_sample, (((1,), (1,)), ((), ())), preferred_el...  79.6 us
    conv_general_dilated x5, matrix products, conv_rows(): lax.conv_general_dilated(padded, weight, (1, 1), ((0, 0), (1, 1)), dimens...  67.2 us
    reduce_sum x4, other arithmetic, attend_step(): attn_prob = jax.nn.softmax(scores, axis=-1).astype(jnp.bfloat16)  56.2 us
  transfers between devices with their start and end apart: 12, of which 10 were waited for; matrix products, arithmetic and copies ran while one was open for 2% of the time, Pallas kernels for 0%

commit v1 on v0

v1 whole, which is shorter than its diff:
```python
import functools
import math

import jax
import jax.numpy as jnp
from jax import lax
from jax.experimental import pallas as pl
from jax.experimental.pallas import tpu as pltpu
from jax.sharding import PartitionSpec as P

F32 = jnp.float32
BF16 = jnp.bfloat16
GROUPS = 32
GN_EPS = 1e-6
MESH = pl.DeviceIdType.MESH
B_IN, B_CONV, GAIN, SHIFT, B_ATT, N_PAR = 0, 1, 5, 10, 15, 24


def group_total(x_val, steps):
    lane = lax.broadcasted_iota(jnp.int32, x_val.shape, 1)
    width = x_val.shape[1]
    for step in steps:
        above = pltpu.roll(x_val, width - step, 1)
        below = pltpu.roll(x_val, step, 1)
        x_val = x_val + jnp.where((lane & step) == 0, above, below)
    return x_val


def body(cfg, zcol, w_in, par, bk_col, w_conv, w_att, out, hbuf, tbuf, u3, wbuf, wabuf, halo, stat_src, stat_rcv,
         ring, qbuf, acc, mx, ls, nbuf, kt, vbuf, obuf, osend,
         w_sem, wa_sem, st_send, st_recv, ha_send, ha_recv, rg_send, rg_recv, sw_send, sw_recv, o_send, o_recv, out_sem):
    n_dev, n_rows, width, n_chan = cfg
    n_tok = n_rows * width
    lanes = n_chan // GROUPS
    n_vreg = n_chan // 128
    count = n_dev * n_tok * lanes
    me = lax.axis_index('cp')
    core = lax.rem(me, 2)
    mate = me + 1 - 2 * core
    ahead = lax.rem(me + 2, n_dev)
    behind = lax.rem(me + n_dev - 2, n_dev)
    below = lax.rem(me + 1, n_dev)
    above = lax.rem(me + n_dev - 1, n_dev)

    barrier = pltpu.get_barrier_semaphore()
    for dist in range(1, n_dev):
        pl.semaphore_signal(barrier, inc=1, device_id={'cp': lax.rem(me + dist, n_dev)}, device_id_type=MESH)

    def load_weights(idx):
        return pltpu.make_async_copy(w_conv.at[idx], wbuf.at[idx % 2], w_sem.at[idx % 2])

    load_weights(0).start()
    load_weights(1).start()
    load_att = pltpu.make_async_copy(w_att, wabuf, wa_sem)
    load_att.start()

    def row_of(idx):
        return par[pl.ds(idx, 1), :]

    def remote(src, dst, send_sem, recv_sem, dev):
        return pltpu.make_async_remote_copy(src_ref=src, dst_ref=dst, send_sem=send_sem, recv_sem=recv_sem,
                                            device_id={'cp': dev}, device_id_type=MESH)

    def partial(val):
        parts = val.reshape(val.shape[0] // 8, 8, n_chan)
        return jnp.sum(parts, axis=0), jnp.sum(parts * parts, axis=0)

    def send_stats(exch, smp, sums):
        row = lax.broadcasted_iota(jnp.int32, (8, n_chan), 0)
        first = jnp.sum(sums[0], axis=0, keepdims=True)
        second = jnp.sum(sums[1], axis=0, keepdims=True)
        both = jnp.where(row == 0, first, jnp.where(row == 1, second, 0.0))
        both = group_total(both, (1, 2, 4, 8))
        lane = lax.broadcasted_iota(jnp.int32, (8, 128), 1)
        packed = both[:, :128]
        for idx in range(1, n_vreg):
            packed = jnp.where((lane & 3) == idx, both[:, idx * 128:(idx + 1) * 128], packed)
        stat_src[exch, smp] = packed
        for dist in range(1, n_dev):
            remote(stat_src.at[exch, smp], stat_rcv.at[exch, smp, dist - 1], st_send.at[exch, smp],
                   st_recv.at[exch, smp], lax.rem(me + dist, n_dev)).start()

    def wait_stats(exch, smp):
        every = stat_rcv.at[exch, smp]
        pltpu.make_async_copy(every, every, st_recv.at[exch, smp]).wait()
        pltpu.make_async_copy(every, every, st_send.at[exch, smp]).wait()

    def affine(exch, smp, norm):
        total = stat_src[exch, smp] + jnp.sum(stat_rcv[exch, smp], axis=0)
        lane = lax.broadcasted_iota(jnp.int32, (8, 128), 1)
        spread = [group_total(jnp.where((lane & 3) == idx, total, 0.0), (1, 2)) for idx in range(n_vreg)]
        full = jnp.concatenate(spread, axis=1)
        mean = full[0:1, :] / count
        inv = lax.rsqrt(full[1:2, :] / count - mean * mean + GN_EPS)
        mul = inv * row_of(GAIN + norm)
        return mul, row_of(SHIFT + norm) - mean * mul

    def halo_copies(exch, smp, buf):
        top = remote(buf.at[smp, pl.ds(0, width)], halo.at[exch, smp, 1], ha_send.at[exch, smp, 0], ha_recv.at[exch, smp, 1], above)
        bottom = remote(buf.at[smp, pl.ds(n_tok - width, width)], halo.at[exch, smp, 0], ha_send.at[exch, smp, 1], ha_recv.at[exch, smp, 0], below)
        return top, bottom

    def send_halo(exch, smp, buf):
        for copy in halo_copies(exch, smp, buf):
            copy.start()

    def wait_halo(exch, smp, buf):
        for copy in halo_copies(exch, smp, buf):
            copy.wait()

    def conv_sample(smp, conv, norm, exch, hexch, src, dst, res):
        wait_stats(exch, smp)
        wait_halo(hexch, smp, src)
        mul, add = affine(exch, smp, norm)
        col = lax.broadcasted_iota(jnp.int32, (width, n_chan), 0)

        def put(row, x_val, keep):
            y_val = x_val.astype(F32) * mul + add
            half = 0.5 * y_val
            act = half + half * jnp.tanh(half)
            if keep is not None:
                act = jnp.where(keep, act, 0.0)
            left = jnp.where(col == 0, 0.0, pltpu.roll(act, 1, 0))
            right = jnp.where(col == width - 1, 0.0, pltpu.roll(act, width - 1, 0))
            u3[pl.ds(row * width, width), :n_chan] = left.astype(BF16)
            u3[pl.ds(row * width, width), n_chan:2 * n_chan] = act.astype(BF16)
            u3[pl.ds(row * width, width), 2 * n_chan:] = right.astype(BF16)

        put(0, halo[hexch, smp, 0], me > 0)
        put(n_rows + 1, halo[hexch, smp, 1], me < n_dev - 1)

        def put_row(row, carry):
            put(row + 1, src[smp, pl.ds(row * width, width), :], None)
            return carry

        lax.fori_loop(0, n_rows, put_row, 0)
        span = n_tok // 2
        bias = row_of(B_CONV + conv)
        taps = 3 * n_chan

        def block(idx, sums):
            base = idx * span
            total = bias
            for dy in range(3):
                total = total + jnp.dot(u3[pl.ds(base + dy * width, span), :], wbuf[conv % 2, dy * taps:(dy + 1) * taps, :],
                                        preferred_element_type=F32)
            if res is not None:
                total = total + res[smp, pl.ds(base, span), :].astype(F32)
            rounded = total.astype(BF16)
            dst[smp, pl.ds(base, span), :] = rounded
            one, two = partial(rounded.astype(F32))
            return sums[0] + one, sums[1] + two

        zero = jnp.zeros((8, n_chan), F32)
        return lax.fori_loop(0, 2, block, (zero, zero))

    def first(smp, carry):
        total = jnp.dot(zcol[smp], w_in[...], preferred_element_type=F32) + row_of(B_IN)
        rounded = total.astype(BF16)
        hbuf[smp] = rounded

        @pl.when(smp == 0)
        def _():
            pl.semaphore_wait(barrier, n_dev - 1)

        send_halo(0, smp, hbuf)
        send_stats(0, smp, partial(rounded.astype(F32)))
        return carry

    lax.fori_loop(0, 2, first, 0)

    load_weights(0).wait()

    def stage0(smp, carry):
        sums = conv_sample(smp, 0, 0, 0, 0, hbuf, tbuf, None)
        send_halo(1, smp, tbuf)
        send_stats(1, smp, sums)
        return carry

    lax.fori_loop(0, 2, stage0, 0)
    load_weights(2).start()
    load_weights(1).wait()

    def forward(idx):
        return remote(ring.at[idx], ring.at[idx + 2], rg_send.at[0, idx], rg_recv.at[idx + 2], ahead)

    def backward(idx):
        src = 1 - idx if isinstance(idx, int) and idx < 2 else idx + 7
        return remote(ring.at[src], ring.at[idx + 9], rg_send.at[1, idx], rg_recv.at[idx + 9], behind)

    def swap():
        return remote(hbuf.at[1 - core], ring.at[1], sw_send, sw_recv, mate)

    def stage1(smp, carry):
        sums = conv_sample(smp, 1, 1, 1, 1, tbuf, hbuf, hbuf)
        send_stats(2, smp, sums)

        @pl.when(smp == 1 - core)
        def _():
            swap().start()

        @pl.when(smp == core)
        def _():
            ring[0] = hbuf[smp]
            forward(0).start()

        return carry

    lax.fori_loop(0, 2, stage1, 0)
    load_weights(3).start()
    backward(1).start()
    swap().wait()
    forward(1).start()
    backward(0).start()
    load_att.wait()

    wait_stats(2, core)
    wait_stats(2, 1 - core)
    mul2, add2 = affine(2, core, 2)
    scale = n_chan ** -0.5 * math.log2(math.e)
    mx[...] = jnp.full(mx.shape, -jnp.inf, F32)
    ls[...] = jnp.zeros(ls.shape, F32)
    acc[...] = jnp.zeros(acc.shape, F32)

    def norm_slot(slot):
        nbuf[...] = (ring[slot].astype(F32) * mul2 + add2).astype(BF16)

    def query(slot, carry):
        norm_slot(slot)
        proj = jnp.dot(nbuf[...], wabuf[0], preferred_element_type=F32) + row_of(B_ATT)
        qbuf[pl.ds(slot * n_tok, n_tok), :] = proj.astype(BF16)
        return carry

    lax.fori_loop(0, 2, query, 0)
    q_len = n_tok // 2

    def attend(slot):
        norm_slot(slot)
        keys = lax.dot_general(wabuf[1], nbuf[...], (((1,), (1,)), ((), ())), preferred_element_type=F32)
        kt[...] = (keys + bk_col[:, 0:1]).astype(BF16)
        vals = jnp.dot(nbuf[...], wabuf[2], preferred_element_type=F32) + row_of(B_ATT + 2)
        vbuf[...] = vals.astype(BF16)

        def one(blk, carry):
            rows = pl.ds(blk * q_len, q_len)
            scores = jnp.dot(qbuf[rows, :], kt[...], preferred_element_type=F32)
            old = mx[rows, :]
            new = jnp.maximum(old, jnp.max(scores, axis=1, keepdims=True) * scale)
            fade = jnp.exp2(old - new)
            prob = jnp.exp2(scores * scale - new[:, 0:1])
            mx[rows, :] = new
            ls[rows, :] = ls[rows, :] * fade + jnp.sum(prob, axis=1, keepdims=True)
            acc[rows, :] = acc[rows, :] * fade[:, 0:1] + jnp.dot(prob.astype(BF16), vbuf[...], preferred_element_type=F32)
            return carry

        lax.fori_loop(0, 4, one, 0)

    def own(slot, carry):
        attend(slot)
        return carry

    lax.fori_loop(0, 2, own, 0)

    def step(idx, carry):
        forward(idx - 1).wait_recv()

        @pl.when(idx <= 5)
        def _():
            forward(idx + 1).start()

        remote(ring.at[idx + 8], ring.at[idx + 8], rg_send.at[1, idx - 1], rg_recv.at[idx + 8], behind).wait_recv()

        @pl.when(idx <= 5)
        def _():
            backward(idx + 1).start()

        def both(side, inner):
            attend(idx + 1 + 7 * side)
            return inner

        return lax.fori_loop(0, 2, both, carry)

    lax.fori_loop(1, 8, step, 0)

    def drain(idx, carry):
        forward(idx).wait_send()
        remote(ring.at[0], ring.at[9], rg_send.at[1, idx], rg_recv.at[9], behind).wait_send()
        return carry

    lax.fori_loop(0, 7, drain, 0)

    osend[...] = (acc[n_tok:, :] / ls[n_tok:, 0:1]).astype(BF16)
    give = remote(osend, obuf.at[1], o_send, o_recv, mate)
    give.start()
    obuf[0] = (acc[:n_tok, :] / ls[:n_tok, 0:1]).astype(BF16)

    def project(side, carry):
        @pl.when(side == 1)
        def _():
            give.wait()

        smp = lax.rem(core + side, 2)
        total = jnp.dot(obuf[side], wabuf[3], preferred_element_type=F32) + row_of(B_ATT + 3)
        rounded = (hbuf[smp].astype(F32) + total).astype(BF16)
        hbuf[smp] = rounded
        send_halo(2, smp, hbuf)
        send_stats(3, smp, partial(rounded.astype(F32)))
        return carry

    lax.fori_loop(0, 2, project, 0)
    load_weights(2).wait()

    def stage2(smp, carry):
        sums = conv_sample(smp, 2, 3, 3, 2, hbuf, tbuf, None)
        send_halo(3, smp, tbuf)
        send_stats(4, smp, sums)
        return carry

    lax.fori_loop(0, 2, stage2, 0)
    load_weights(3).wait()

    def write(smp):
        return pltpu.make_async_copy(tbuf.at[smp], out.at[smp], out_sem.at[smp])

    def stage3(smp, carry):
        conv_sample(smp, 3, 4, 4, 3, tbuf, tbuf, hbuf)
        write(smp).start()
        return carry

    lax.fori_loop(0, 2, stage3, 0)
    write(0).wait()
    write(1).wait()


def decoder(n_dev, zcol, w_in, par, bk_col, w_conv, w_att, n_rows, width):
    n_chan = w_in.shape[1]
    n_tok = n_rows * width
    vmem = pltpu.VMEM
    dma = pltpu.SemaphoreType.DMA
    in_vmem = pl.BlockSpec(memory_space=pltpu.VMEM)
    in_any = pl.BlockSpec(memory_space=pl.ANY)
    scratch = [
        vmem((2, n_tok, n_chan), BF16),
        vmem((2, n_tok, n_chan), BF16),
        vmem((n_tok + 2 * width, 3 * n_chan), BF16),
        vmem((2, 9 * n_chan, n_chan), BF16),
        vmem((4, n_chan, n_chan), BF16),
        vmem((4, 2, 2, width, n_chan), BF16),
        vmem((5, 2, 8, 128), F32),
        vmem((5, 2, n_dev - 1, 8, 128), F32),
        vmem((n_dev, n_tok, n_chan), BF16),
        vmem((2 * n_tok, n_chan), BF16),
        vmem((2 * n_tok, n_chan), F32),
        vmem((2 * n_tok, 128), F32),
        vmem((2 * n_tok, 128), F32),
        vmem((n_tok, n_chan), BF16),
        vmem((n_chan, n_tok), BF16),
        vmem((n_tok, n_chan), BF16),
        vmem((2, n_tok, n_chan), BF16),
        vmem((n_tok, n_chan), BF16),
        dma((2,)), dma, dma((5, 2)), dma((5, 2)), dma((4, 2, 2)), dma((4, 2, 2)), dma((2, 7)), dma((16,)),
        dma, dma, dma, dma, dma((2,)),
    ]
    return pl.pallas_call(
        functools.partial(body, (n_dev, n_rows, width, n_chan)),
        out_shape=jax.ShapeDtypeStruct((2, n_tok, n_chan), BF16),
        in_specs=[in_vmem, in_vmem, in_vmem, in_vmem, in_any, in_any],
        out_specs=in_any,
        scratch_shapes=scratch,
        compiler_params=pltpu.CompilerParams(collective_id=0, has_side_effects=True, vmem_limit_bytes=67043328),
    )(zcol, w_in, par, bk_col, w_conv, w_att)


def solution(mesh):
    n_dev = mesh.shape['cp']

    def local_fn(latents, w_in, b_in, w_conv, b_conv, gn_scale, gn_shift, w_attn, b_attn):
        n_batch, n_rows, width, n_z = latents.shape
        n_chan = w_in.shape[-1]
        down_pairs = [(sender, sender + 1) for sender in range(n_dev - 1)]
        up_pairs = [(sender + 1, sender) for sender in range(n_dev - 1)]
        from_above = lax.ppermute(latents[:, -1:], 'cp', down_pairs)
        from_below = lax.ppermute(latents[:, :1], 'cp', up_pairs)
        padded = jnp.concatenate([from_above, latents, from_below], axis=1)
        padded = jnp.pad(padded, ((0, 0), (0, 0), (1, 1), (0, 0)))
        taps = [padded[:, dy:dy + n_rows, dx:dx + width] for dy in range(3) for dx in range(3)]
        taps.append(jnp.zeros((n_batch, n_rows, width, 128 - 9 * n_z), BF16))
        zcol = jnp.concatenate(taps, axis=-1).reshape(n_batch, n_rows * width, 128)
        w_first = jnp.pad(w_in.reshape(9 * n_z, n_chan), ((0, 128 - 9 * n_z), (0, 0)))
        par = jnp.concatenate([b_in[None], b_conv, gn_scale, gn_shift, b_attn]).astype(F32)
        par = jnp.pad(par, ((0, N_PAR - par.shape[0]), (0, 0)))
        bk_col = jnp.broadcast_to(b_attn[1].astype(F32)[:, None], (n_chan, 128))
        w_att = jnp.stack([w_attn[0], w_attn[1].T, w_attn[2], w_attn[3]])
        out = decoder(n_dev, zcol, w_first, par, bk_col, w_conv.reshape(4, 9 * n_chan, n_chan), w_att, n_rows, width)
        return out.reshape(n_batch, n_rows, width, n_chan)

    band_spec = P('dp', 'cp')
    whole_spec = P()
    return jax.shard_map(local_fn, mesh=mesh, in_specs=(band_spec,) + (whole_spec,) * 8, out_specs=band_spec, check_vma=False)
```

time: 982 us -> 300 us (0.31); the launches traced: 970 us -> 299 us
  waiting for transfers between devices: 354 us -> 0.01 us
  Pallas kernels: 0 us -> 268 us
  matrix products: 247 us -> 0 us
  blocking collectives: 117 us -> 0 us
  other arithmetic: 117 us -> 2.26 us
  local copies, waits for them, and re-layouts: 88.6 us -> 21.3 us
  starting transfers between devices: 32.2 us -> 7.89 us
  between operations: 14.6 us -> 0.14 us
    all_gather x2 -> x0, waiting for transfers between devices: 341 us -> none  [the longest x1 171 us: local_fn(): vals_all = lax.all_gather(project(2), 'cp', axis=1, tiled=True)]
    pallas_call x0 -> x1, Pallas kernels: none -> 268 us  [decoder(): pl.pallas_call(functools.partial(body, (n_dev, n_rows, width, n_chan)), o...]
    dot_general x12 -> x0, matrix products: 179 us -> none  [the longest x4 85.8 us: attend_step(): jnp.dot(attn_prob, v_sample, preferred_element_type=jnp.float32)]
    psum x5 -> x0, blocking collectives: 117 us -> none  [group_norm(): totals = lax.psum(local_sums, 'cp')]
    conv_general_dilated x5 -> x0, matrix products: 67.2 us -> none  [conv_rows(): lax.conv_general_dilated(padded, weight, (1, 1), ((0, 0), (1, 1)), dimens...]
    reduce_sum x23 -> x0, other arithmetic: 62.4 us -> none  [the longest x4 56.2 us: attend_step(): attn_prob = jax.nn.softmax(scores, axis=-1).astype(jnp.bfloat16)]
    convert_element_type x10 -> x1, other arithmetic: 28.3 us -> 0.01 us  [local_fn(): bk_col = jnp.broadcast_to(b_attn[1].astype(F32)[:, None], (n_chan, 128))]
    ppermute x10 -> x2, starting transfers between devices: 32.1 us -> 7.89 us  [the longest x1 5.09 us: local_fn(): from_above = lax.ppermute(latents[:, -1:], 'cp', down_pairs)]
  transfers between devices with their start and end apart: 12 -> 2, of which waited for: 10 -> 0; matrix products, arithmetic and copies ran while one was open for 2% -> 2% of each run, Pallas kernels for 0% -> 0%
where the time goes in v1:
time: 300 us; the launch traced here: 299 us
  Pallas kernels  268 us (89%)
  local copies, waits for them, and re-layouts  21.3 us (7%)
  starting transfers between devices  7.89 us (3%)
    pallas_call x1, Pallas kernels, decoder(): pl.pallas_call(functools.partial(body, (n_dev, n_rows, width, n_chan)), o...  268 us
    concatenate x1, local copies, waits for them, and re-layouts, local_fn(): zcol = jnp.concatenate(taps, axis=-1).reshape(n_batch, n_rows * width, 128)  7.06 us
  transfers between devices with their start and end apart: 2, of which 0 were waited for; matrix products, arithmetic and copies ran while one was open for 2% of the time, Pallas kernels for 0%

profile of v1, /device:TPU:21, one launch (start us, length us, event | category | flops | bytes accessed | tf_op | source)
XLA Modules:
  0.0 299.5 jit_solution(13633884353055051404)
XLA Ops:
  0.0 0.7 fusion.3
  0.7 5.1 %collective-permute-start = (bf16[2,1,128,4]{2,3,1,0:T(4,128)(2,1)S(1)}, bf16[2,1,128,4]{2,3,1,0:T(4,128)(2,1)S(1)}, u32[]{:S(2)}, u32[]{:S(2)}) collective-permute-start(bf16[2,1,128,4]{2,3,1,0:T(4,128)(2,1)S(1)} %get-tuple-element.15), channel_id=1, source_target_pairs={{0,1},{1,2},{2,3},{3,4},{4,5},{5,6},{6,7},{7,8},{8,9},{9,10},{10,1... | collective-permute-start | bytes 6152 | tf_op jit(solution)/shard_map/ppermute | solution.py:382
  5.8 2.8 collective-permute-start.1
  8.6 1.3 fusion.1
  9.9 0.0 copy-start.2
  9.9 0.0 copy-start.6
  9.9 0.0 slice-start
  9.9 0.2 copy.20
  10.1 0.4 copy-done.2
  10.6 0.0 copy-done.6
  10.6 0.5 slice-done
  11.1 0.0 copy-start.3
  11.1 0.0 copy-start.4
  11.1 0.0 copy-start.5
  11.1 0.0 copy-start
  11.2 0.0 copy-start.1
  11.2 1.5 pad_maximum_fusion.w_att
  12.7 0.0 copy-done.3
  12.7 0.0 copy-done.4
  12.7 0.0 copy-done.5
  12.7 0.2 concatenate.19
  12.9 0.6 pad_convert_fusion.par
  13.5 0.0 copy-done
  13.6 0.3 copy.14
  13.9 0.0 copy-done.1
  13.9 0.7 pad.15.w_in
  14.6 0.0 collective-permute-done
  14.6 0.0 collective-permute-done.1
  14.6 0.1 select_maximum_fusion
  14.7 0.1 fusion.2
  14.8 0.3 copy.10
  15.1 0.3 copy.12
  15.4 0.3 copy.13
  15.8 0.3 copy.15
  16.1 0.3 copy.16
  16.4 1.1 copy.18
  17.5 1.1 copy.11
  18.6 1.1 copy.17
  19.7 0.9 broadcast_in_dim.12
  20.6 7.1 %concatenate.18 = bf16[2,8,128,128]{3,2,1,0:T(8,128)(2,1)} concatenate(bf16[2,8,128,4]{3,2,1,0:T(8,128)(2,1)S(1)} %copy.10, bf16[2,8,128,4]{3,2,1,0:T(8,128)(2,1)} %copy.11, bf16[2,8,128,4]{3,2,1,0:T(8,128)(2,1)S(1)} %copy.12, bf16[2,8,128,4]{3,2,1,0:T(8,128)(2,1)S(1)} %copy.13, bf16[2,8,128,4]{3,2,1,0:T(8,128)(2,1)S(1)} %copy.14, bf16[2,8,128,4]{3,2,1,0:T(8,128)(2,1)S(1)} %copy.15, ...), dimensions={3} | concatenate | bytes 1048576 | tf_op jit(solution)/shard_map/concatenate | solution.py:388
  27.6 0.8 broadcast_in_dim.14.bk_col
  28.5 267.9 %shard_map.91 = bf16[2,1024,512]{2,1,0:T(8,128)(2,1)} custom-call(bf16[2,1024,128]{2,1,0:T(8,128)(2,1)} %bitcast.11, bf16[128,512]{1,0:T(8,128)(2,1)} %pad.15.w_in, f32[24,512]{1,0:T(8,128)} %pad_convert_fusion.par, f32[512,128]{1,0:T(8,128)} %broadcast_in_dim.14.bk_col, bf16[4,4608,512]{2,1,0:T(8,128)(2,1)} %bitcast.9, ...), custom_call_target="tpu_custom_call" | custom-call | tf_op jit(solution)/shard_map/pallas_call | solution.py:364
  296.4 3.1 %copy.22 = bf16[2,8,128,512]{3,2,1,0:T(8,128)(2,1)} copy(bf16[2,8,128,512]{3,2,1,0:T(8,128)(2,1)} %bitcast.10) | data formatting | bytes 4194304
  (4 shorter events, 0.0 us)
Async XLA Ops:
  0.7 13.9 %collective-permute-start = (bf16[2,1,128,4]{2,3,1,0:T(4,128)(2,1)S(1)}, bf16[2,1,128,4]{2,3,1,0:T(4,128)(2,1)S(1)}, u32[]{:S(2)}, u32[]{:S(2)}) collective-permute-start(bf16[2,1,128,4]{2,3,1,0:T(4,128)(2,1)S(1)} %get-tuple-element.15), channel_id=1, source_target_pairs={{0,1},{1,2},{2,3},{3,4},{4,5},{5,6},{6,7},{7,8},{8,9},{9,10},{10,1... | collective-permute-start | bytes 6152 | tf_op jit(solution)/shard_map/ppermute | solution.py:382
  5.8 8.8 %collective-permute-start.1 = (bf16[2,1,128,4]{2,3,1,0:T(4,128)(2,1)S(1)}, bf16[2,1,128,4]{2,3,1,0:T(4,128)(2,1)S(1)}, u32[]{:S(2)}, u32[]{:S(2)}) collective-permute-start(bf16[2,1,128,4]{2,3,1,0:T(4,128)(2,1)S(1)} %get-tuple-element.16), channel_id=1, source_target_pairs={{1,0},{2,1},{3,2},{4,3},{5,4},{6,5},{7,6},{8,7},{9,8},{10,9},{11,1... | collective-permute-start | bytes 6152 | tf_op jit(solution)/shard_map/ppermute | solution.py:383
  9.9 0.7 copy-start.2
  9.9 0.7 copy-start.6
  9.9 1.2 slice-start
  11.1 1.6 copy-start.3
  11.1 1.6 copy-start.4
  11.1 1.6 copy-start.5
  11.1 2.4 copy-start
  11.2 2.7 copy-start.1

commit v2 on v1

--- a/solution.py
+++ b/solution.py
@@ -26,9 +26,9 @@
     return x_val
 
 
-def body(cfg, zcol, w_in, par, bk_col, w_conv, w_att, out, hbuf, tbuf, u3, wbuf, wabuf, halo, stat_src, stat_rcv,
-         ring, qbuf, acc, mx, ls, nbuf, kt, vbuf, obuf, osend,
-         w_sem, wa_sem, st_send, st_recv, ha_send, ha_recv, rg_send, rg_recv, sw_send, sw_recv, o_send, o_recv, out_sem):
+def body(cfg, lat, w_in, b_in, b_conv, gain, shift, b_att, w_conv, w_att, out, hbuf, tbuf, u3, wbuf, wabuf, halo, stat_src, stat_rcv,
+         ring, qbuf, acc, mx, ls, nbuf, kt, vbuf, obuf, par, bk_col, w_first, z_src, z_halo, z_col, z_tok,
+         w_sem, wa_sem, st_send, st_recv, ha_send, ha_recv, rg_send, rg_recv, sw_send, sw_recv, o_send, o_recv, out_sem, z_send, z_recv):
     n_dev, n_rows, width, n_chan = cfg
     n_tok = n_rows * width
     lanes = n_chan // GROUPS
@@ -53,6 +53,13 @@
     load_weights(1).start()
     load_att = pltpu.make_async_copy(w_att, wabuf, wa_sem)
     load_att.start()
+
+    par[...] = jnp.zeros(par.shape, F32)
+    par[B_IN:B_IN + 1, :] = b_in[...].astype(F32)
+    par[B_CONV:B_CONV + 4, :] = b_conv[...].astype(F32)
+    par[GAIN:GAIN + 5, :] = gain[...].astype(F32)
+    par[SHIFT:SHIFT + 5, :] = shift[...].astype(F32)
+    par[B_ATT:B_ATT + 4, :] = b_att[...].astype(F32)
 
     def row_of(idx):
         return par[pl.ds(idx, 1), :]
@@ -126,43 +133,71 @@
             u3[pl.ds(row * width, width), n_chan:2 * n_chan] = act.astype(BF16)
             u3[pl.ds(row * width, width), 2 * n_chan:] = right.astype(BF16)
 
-        put(0, halo[hexch, smp, 0], me > 0)
-        put(n_rows + 1, halo[hexch, smp, 1], me < n_dev - 1)
-
         def put_row(row, carry):
             put(row + 1, src[smp, pl.ds(row * width, width), :], None)
             return carry
 
-        lax.fori_loop(0, n_rows, put_row, 0)
-        span = n_tok // 2
+        put(0, halo[hexch, smp, 0], me > 0)
+        half_rows = n_rows // 2
+        lax.fori_loop(0, half_rows + 1, put_row, 0)
+        span = half_rows * width
         bias = row_of(B_CONV + conv)
         taps = 3 * n_chan
-
-        def block(idx, sums):
+        sums = [jnp.zeros((8, n_chan), F32)] * 2
+        for idx in range(2):
             base = idx * span
             total = bias
             for dy in range(3):
-                total = total + jnp.dot(u3[pl.ds(base + dy * width, span), :], wbuf[conv % 2, dy * taps:(dy + 1) * taps, :],
-                                        preferred_element_type=F32)
+                start = base + dy * width
+                total = total + jnp.dot(u3[start:start + span, :], wbuf[conv % 2, dy * taps:(dy + 1) * taps, :], preferred_element_type=F32)
+            if idx == 0:
+                for row in range(half_rows + 1, n_rows):
+                    put_row(row, 0)
+                put(n_rows + 1, halo[hexch, smp, 1], me < n_dev - 1)
             if res is not None:
-                total = total + res[smp, pl.ds(base, span), :].astype(F32)
+                total = total + res[smp, base:base + span, :].astype(F32)
             rounded = total.astype(BF16)
-            dst[smp, pl.ds(base, span), :] = rounded
-            one, two = partial(rounded.astype(F32))
-            return sums[0] + one, sums[1] + two
-
-        zero = jnp.zeros((8, n_chan), F32)
-        return lax.fori_loop(0, 2, block, (zero, zero))
+            dst[smp, base:base + span, :] = rounded
+            sums = [old + new for old, new in zip(sums, partial(rounded.astype(F32)))]
+        return sums
+
+    n_z = lat.shape[2]
+    rows = [jnp.concatenate([lat[0, row].astype(F32), lat[1, row].astype(F32)], axis=0) for row in range(n_rows)]
+    z_src[0] = rows[0]
+    z_src[1] = rows[-1]
+    blank = jnp.zeros((n_z, n_chan), F32)
+    for smp in range(2):
+        pieces = []
+        for tap in range(9):
+            pair = [blank, blank]
+            pair[smp] = w_in[tap].astype(F32)
+            pieces += pair
+        pieces.append(jnp.zeros((128 - 18 * n_z, n_chan), F32))
+        w_first[smp] = jnp.concatenate(pieces, axis=0).astype(BF16)
+    pl.semaphore_wait(barrier, n_dev - 1)
+    z_copies = (remote(z_src.at[0], z_halo.at[1], z_send.at[0], z_recv.at[1], above),
+                remote(z_src.at[1], z_halo.at[0], z_send.at[1], z_recv.at[0], below))
+    for copy in z_copies:
+        copy.start()
+    for copy in z_copies:
+        copy.wait()
+    rows = [jnp.where(me > 0, z_halo[0], 0.0)] + rows + [jnp.where(me < n_dev - 1, z_halo[1], 0.0)]
+    lane = lax.broadcasted_iota(jnp.int32, (2 * n_z, width), 1)
+    for tap in range(9):
+        dy, dx = tap // 3, tap % 3
+        moved = rows[dy:dy + n_rows]
+        if dx == 0:
+            moved = [jnp.where(lane == 0, 0.0, pltpu.roll(row, 1, 1)) for row in moved]
+        if dx == 2:
+            moved = [jnp.where(lane == width - 1, 0.0, pltpu.roll(row, width - 1, 1)) for row in moved]
+        z_col[tap * 2 * n_z:(tap + 1) * 2 * n_z, :] = jnp.concatenate(moved, axis=1)
+    z_col[18 * n_z:, :] = jnp.zeros((128 - 18 * n_z, n_tok), F32)
+    z_tok[...] = jnp.transpose(z_col[...]).astype(BF16)
 
     def first(smp, carry):
-        total = jnp.dot(zcol[smp], w_in[...], preferred_element_type=F32) + row_of(B_IN)
+        total = jnp.dot(z_tok[...], w_first[smp], preferred_element_type=F32) + row_of(B_IN)
         rounded = total.astype(BF16)
         hbuf[smp] = rounded
-
-        @pl.when(smp == 0)
-        def _():
-            pl.semaphore_wait(barrier, n_dev - 1)
-
         send_halo(0, smp, hbuf)
         send_stats(0, smp, partial(rounded.astype(F32)))
         return carry
@@ -203,16 +238,18 @@
         def _():
             ring[0] = hbuf[smp]
             forward(0).start()
+            backward(1).start()
 
         return carry
 
     lax.fori_loop(0, 2, stage1, 0)
     load_weights(3).start()
-    backward(1).start()
     swap().wait()
     forward(1).start()
     backward(0).start()
     load_att.wait()
+    wabuf[1] = jnp.transpose(wabuf[1].astype(F32)).astype(BF16)
+    bk_col[...] = jnp.transpose(jnp.broadcast_to(row_of(B_ATT + 1), (128, n_chan)))
 
     wait_stats(2, core)
     wait_stats(2, 1 - core)
@@ -241,19 +278,25 @@
         vals = jnp.dot(nbuf[...], wabuf[2], preferred_element_type=F32) + row_of(B_ATT + 2)
         vbuf[...] = vals.astype(BF16)
 
-        def one(blk, carry):
-            rows = pl.ds(blk * q_len, q_len)
-            scores = jnp.dot(qbuf[rows, :], kt[...], preferred_element_type=F32)
+        def score(blk):
+            return jnp.dot(qbuf[blk * q_len:(blk + 1) * q_len, :], kt[...], preferred_element_type=F32)
+
+        n_part = max(n_tok // 128, 1)
+        wide = n_tok // n_part
+        scores = score(0)
+        for blk in range(4):
+            following = score(blk + 1) if blk < 3 else None
+            rows = slice(blk * q_len, (blk + 1) * q_len)
+            cols = [scores[:, idx * wide:(idx + 1) * wide] for idx in range(n_part)]
             old = mx[rows, :]
-            new = jnp.maximum(old, jnp.max(scores, axis=1, keepdims=True) * scale)
+            new = jnp.maximum(old, jnp.max(functools.reduce(jnp.maximum, cols), axis=1, keepdims=True) * scale)
             fade = jnp.exp2(old - new)
-            prob = jnp.exp2(scores * scale - new[:, 0:1])
+            prob = [jnp.exp2(col * scale - new[:, :wide]) for col in cols]
             mx[rows, :] = new
-            ls[rows, :] = ls[rows, :] * fade + jnp.sum(prob, axis=1, keepdims=True)
-            acc[rows, :] = acc[rows, :] * fade[:, 0:1] + jnp.dot(prob.astype(BF16), vbuf[...], preferred_element_type=F32)
-            return carry
-
-        lax.fori_loop(0, 4, one, 0)
+            ls[rows, :wide] = ls[rows, :wide] * fade[:, :wide] + functools.reduce(jnp.add, prob)
+            prob = jnp.concatenate([col.astype(BF16) for col in prob], axis=1)
+            acc[rows, :] = acc[rows, :] * fade[:, 0:1] + jnp.dot(prob, vbuf[...], preferred_element_type=F32)
+            scores = following
 
     def own(slot, carry):
         attend(slot)
@@ -289,10 +332,14 @@
 
     lax.fori_loop(0, 7, drain, 0)
 
-    osend[...] = (acc[n_tok:, :] / ls[n_tok:, 0:1]).astype(BF16)
-    give = remote(osend, obuf.at[1], o_send, o_recv, mate)
+    def finish(base):
+        total = jnp.sum(ls[base:base + n_tok, :], axis=1, keepdims=True)
+        return (acc[base:base + n_tok, :] / total).astype(BF16)
+
+    vbuf[...] = finish(n_tok)
+    give = remote(vbuf, obuf.at[1], o_send, o_recv, mate)
     give.start()
-    obuf[0] = (acc[:n_tok, :] / ls[:n_tok, 0:1]).astype(BF16)
+    obuf[0] = finish(0)
 
     def project(side, carry):
         @pl.when(side == 1)
@@ -332,8 +379,9 @@
     write(1).wait()
 
 
-def decoder(n_dev, zcol, w_in, par, bk_col, w_conv, w_att, n_rows, width):
-    n_chan = w_in.shape[1]
+def decoder(n_dev, lat, w_in, b_in, b_conv, gain, shift, b_att, w_conv, w_att):
+    n_rows, n_z, width = lat.shape[1:]
+    n_chan = w_in.shape[-1]
     n_tok = n_rows * width
     vmem = pltpu.VMEM
     dma = pltpu.SemaphoreType.DMA
@@ -357,18 +405,24 @@
         vmem((n_chan, n_tok), BF16),
         vmem((n_tok, n_chan), BF16),
         vmem((2, n_tok, n_chan), BF16),
-        vmem((n_tok, n_chan), BF16),
+        vmem((N_PAR, n_chan), F32),
+        vmem((n_chan, 128), F32),
+        vmem((2, 128, n_chan), BF16),
+        vmem((2, 2 * n_z, width), F32),
+        vmem((2, 2 * n_z, width), F32),
+        vmem((128, n_tok), F32),
+        vmem((n_tok, 128), BF16),
         dma((2,)), dma, dma((5, 2)), dma((5, 2)), dma((4, 2, 2)), dma((4, 2, 2)), dma((2, 7)), dma((16,)),
-        dma, dma, dma, dma, dma((2,)),
+        dma, dma, dma, dma, dma((2,)), dma((2,)), dma((2,)),
     ]
     return pl.pallas_call(
         functools.partial(body, (n_dev, n_rows, width, n_chan)),
         out_shape=jax.ShapeDtypeStruct((2, n_tok, n_chan), BF16),
-        in_specs=[in_vmem, in_vmem, in_vmem, in_vmem, in_any, in_any],
+        in_specs=[in_vmem] * 7 + [in_any] * 2,
         out_specs=in_any,
         scratch_shapes=scratch,
         compiler_params=pltpu.CompilerParams(collective_id=0, has_side_effects=True, vmem_limit_bytes=67043328),
-    )(zcol, w_in, par, bk_col, w_conv, w_att)
+    )(lat, w_in, b_in, b_conv, gain, shift, b_att, w_conv, w_att)
 
 
 def solution(mesh):
@@ -377,21 +431,8 @@
     def local_fn(latents, w_in, b_in, w_conv, b_conv, gn_scale, gn_shift, w_attn, b_attn):
         n_batch, n_rows, width, n_z = latents.shape
         n_chan = w_in.shape[-1]
-        down_pairs = [(sender, sender + 1) for sender in range(n_dev - 1)]
-        up_pairs = [(sender + 1, sender) for sender in range(n_dev - 1)]
-        from_above = lax.ppermute(latents[:, -1:], 'cp', down_pairs)
-        from_below = lax.ppermute(latents[:, :1], 'cp', up_pairs)
-        padded = jnp.concatenate([from_above, latents, from_below], axis=1)
-        padded = jnp.pad(padded, ((0, 0), (0, 0), (1, 1), (0, 0)))
-        taps = [padded[:, dy:dy + n_rows, dx:dx + width] for dy in range(3) for dx in range(3)]
-        taps.append(jnp.zeros((n_batch, n_rows, width, 128 - 9 * n_z), BF16))
-        zcol = jnp.concatenate(taps, axis=-1).reshape(n_batch, n_rows * width, 128)
-        w_first = jnp.pad(w_in.reshape(9 * n_z, n_chan), ((0, 128 - 9 * n_z), (0, 0)))
-        par = jnp.concatenate([b_in[None], b_conv, gn_scale, gn_shift, b_attn]).astype(F32)
-        par = jnp.pad(par, ((0, N_PAR - par.shape[0]), (0, 0)))
-        bk_col = jnp.broadcast_to(b_attn[1].astype(F32)[:, None], (n_chan, 128))
-        w_att = jnp.stack([w_attn[0], w_attn[1].T, w_attn[2], w_attn[3]])
-        out = decoder(n_dev, zcol, w_first, par, bk_col, w_conv.reshape(4, 9 * n_chan, n_chan), w_att, n_rows, width)
+        out = decoder(n_dev, latents.transpose(0, 1, 3, 2), w_in.reshape(9, n_z, n_chan), b_in.reshape(1, n_chan), b_conv, gn_scale,
+                      gn_shift, b_attn, w_conv.reshape(4, 9 * n_chan, n_chan), w_attn)
         return out.reshape(n_batch, n_rows, width, n_chan)
 
     band_spec = P('dp', 'cp')

time: 300 us -> 259 us (0.86)
  local copies, waits for them, and re-layouts: 21.3 us -> 4.35 us
  Pallas kernels: 268 us -> 254 us
  starting transfers between devices: 7.89 us -> 0 us
    pallas_call x1, Pallas kernels: 268 us -> 254 us  [decoder(): pl.pallas_call(functools.partial(body, (n_dev, n_rows, width, n_chan)), o...]
    ppermute x2 -> x0, starting transfers between devices: 7.89 us -> none  [the longest x1 5.09 us: local_fn(): from_above = lax.ppermute(latents[:, -1:], 'cp', down_pairs)]
    slice x13 -> x0, local copies, waits for them, and re-layouts: 7.47 us -> none  [the longest x9 4.95 us: local_fn(): padded[:, dy:dy + n_rows, dx:dx + width]]
    concatenate x2 -> x0, local copies, waits for them, and re-layouts: 7.29 us -> none  [the longest x1 7.06 us: local_fn(): zcol = jnp.concatenate(taps, axis=-1).reshape(n_batch, n_rows * width, 128)]
  transfers between devices with their start and end apart: 2 -> 0, of which waited for: 0 -> 0; matrix products, arithmetic and copies ran while one was open for 2% -> 0% of each run, Pallas kernels for 0% -> 0%
where the time goes in v2:
time: 259 us
  Pallas kernels  254 us (98%)
  local copies, waits for them, and re-layouts  4.35 us (2%)
    pallas_call x1, Pallas kernels, decoder(): pl.pallas_call(functools.partial(body, (n_dev, n_rows, width, n_chan)), o...  254 us

profile of v2, /device:TPU:21, one launch (start us, length us, event | category | flops | bytes accessed | tf_op | source)
XLA Modules:
  0.0 258.6 jit_solution(13649945981582031852)
XLA Ops:
  0.0 1.3 reshape.13.b_in
  1.3 254.3 %shard_map.91 = bf16[2,1024,512]{2,1,0:T(8,128)(2,1)} custom-call(bf16[2,8,4,128]{3,2,1,0:T(4,128)(2,1)} %bitcast.7, bf16[9,4,512]{2,1,0:T(4,128)(2,1)} %bitcast.6, bf16[1,512]{1,0:T(2,128)(2,1)} %reshape.13.b_in, bf16[4,512]{1,0:T(4,128)(2,1)} %b_conv.1, bf16[5,512]{1,0:T(8,128)(2,1)} %gain.1, bf16[5,512]{1,0:T(8,128)(2,1)} %shift.1, bf16[4,512]{1,0:T(4,128)(2,1)} %b_att.1, ...), custom_call_target="tpu_custom_call" | custom-call | tf_op jit(solution)/shard_map/pallas_call | solution.py:418
  255.5 3.1 %copy.11 = bf16[2,8,128,512]{3,2,1,0:T(8,128)(2,1)} copy(bf16[2,8,128,512]{3,2,1,0:T(8,128)(2,1)} %bitcast.5) | data formatting | bytes 4194304

commit v3 on v2

--- a/solution.py
+++ b/solution.py
@@ -27,8 +27,8 @@
 
 
 def body(cfg, lat, w_in, b_in, b_conv, gain, shift, b_att, w_conv, w_att, out, hbuf, tbuf, u3, wbuf, wabuf, halo, stat_src, stat_rcv,
-         ring, qbuf, acc, mx, ls, nbuf, kt, vbuf, obuf, par, bk_col, w_first, z_src, z_halo, z_col, z_tok,
-         w_sem, wa_sem, st_send, st_recv, ha_send, ha_recv, rg_send, rg_recv, sw_send, sw_recv, o_send, o_recv, out_sem, z_send, z_recv):
+         ring, qbuf, acc, mx, ls, nbuf, kt, vbuf, obuf, par, bk_col, w_first, z_src, z_halo, z_col, z_tok, z_far, far_in, far_mid,
+         w_sem, wa_sem, st_send, st_recv, ha_send, ha_recv, rg_send, rg_recv, sw_send, sw_recv, o_send, o_recv, out_sem, z_send, z_recv, zf_send, zf_recv):
     n_dev, n_rows, width, n_chan = cfg
     n_tok = n_rows * width
     lanes = n_chan // GROUPS
@@ -55,7 +55,7 @@
     load_att.start()
 
     par[...] = jnp.zeros(par.shape, F32)
-    par[B_IN:B_IN + 1, :] = b_in[...].astype(F32)
+    par[B_IN:B_IN + 1, :] = b_in[...].astype(F32).reshape(1, n_chan)
     par[B_CONV:B_CONV + 4, :] = b_conv[...].astype(F32)
     par[GAIN:GAIN + 5, :] = gain[...].astype(F32)
     par[SHIFT:SHIFT + 5, :] = shift[...].astype(F32)
@@ -115,15 +115,12 @@
         for copy in halo_copies(exch, smp, buf):
             copy.wait()
 
-    def conv_sample(smp, conv, norm, exch, hexch, src, dst, res):
-        wait_stats(exch, smp)
-        wait_halo(hexch, smp, src)
-        mul, add = affine(exch, smp, norm)
-        col = lax.broadcasted_iota(jnp.int32, (width, n_chan), 0)
-
-        def put(row, x_val, keep):
-            y_val = x_val.astype(F32) * mul + add
-            half = 0.5 * y_val
+    col = lax.broadcasted_iota(jnp.int32, (width, n_chan), 0)
+    taps = 3 * n_chan
+
+    def conv_core(rows_out, edge, load, keep_top, keep_bottom, mul, add, conv, res, store):
+        def put(row, keep):
+            half = 0.5 * (load(row).astype(F32) * mul + add)
             act = half + half * jnp.tanh(half)
             if keep is not None:
                 act = jnp.where(keep, act, 0.0)
@@ -134,15 +131,22 @@
             u3[pl.ds(row * width, width), 2 * n_chan:] = right.astype(BF16)
 
         def put_row(row, carry):
-            put(row + 1, src[smp, pl.ds(row * width, width), :], None)
+            put(row, None)
             return carry
 
-        put(0, halo[hexch, smp, 0], me > 0)
-        half_rows = n_rows // 2
-        lax.fori_loop(0, half_rows + 1, put_row, 0)
+        half_rows = rows_out // 2
+
+        def put_top(row, carry):
+            put(row, keep_top)
+            return carry
+
+        if edge == 1:
+            put(0, keep_top)
+        else:
+            lax.fori_loop(0, edge, put_top, 0)
+        lax.fori_loop(edge, half_rows + 2, put_row, 0)
         span = half_rows * width
         bias = row_of(B_CONV + conv)
-        taps = 3 * n_chan
         sums = [jnp.zeros((8, n_chan), F32)] * 2
         for idx in range(2):
             base = idx * span
@@ -151,15 +155,34 @@
                 start = base + dy * width
                 total = total + jnp.dot(u3[start:start + span, :], wbuf[conv % 2, dy * taps:(dy + 1) * taps, :], preferred_element_type=F32)
             if idx == 0:
-                for row in range(half_rows + 1, n_rows):
-                    put_row(row, 0)
-                put(n_rows + 1, halo[hexch, smp, 1], me < n_dev - 1)
+                for row in range(half_rows + 2, rows_out + 2 - edge):
+                    put(row, None)
+                for row in range(rows_out + 2 - edge, rows_out + 2):
+                    put(row, keep_bottom)
             if res is not None:
-                total = total + res[smp, base:base + span, :].astype(F32)
+                total = total + res(base, span).astype(F32)
             rounded = total.astype(BF16)
-            dst[smp, base:base + span, :] = rounded
+            store(base, span, rounded)
             sums = [old + new for old, new in zip(sums, partial(rounded.astype(F32)))]
         return sums
+
+    def conv_sample(smp, conv, norm, exch, hexch, src, dst, res):
+        wait_stats(exch, smp)
+        wait_halo(hexch, smp, src)
+        mul, add = affine(exch, smp, norm)
+
+        def load(row):
+            if isinstance(row, int) and row == 0:
+                return halo[hexch, smp, 0]
+            if isinstance(row, int) and row == n_rows + 1:
+                return halo[hexch, smp, 1]
+            return src[smp, pl.ds((row - 1) * width, width), :]
+
+        def store(base, span, val):
+            dst[smp, base:base + span, :] = val
+
+        get = None if res is None else lambda base, span: res[smp, base:base + span, :]
+        return conv_core(n_rows, 1, load, me > 0, me < n_dev - 1, mul, add, conv, get, store)
 
     n_z = lat.shape[2]
     rows = [jnp.concatenate([lat[0, row].astype(F32), lat[1, row].astype(F32)], axis=0) for row in range(n_rows)]
@@ -179,20 +202,35 @@
                 remote(z_src.at[1], z_halo.at[0], z_send.at[1], z_recv.at[0], below))
     for copy in z_copies:
         copy.start()
+    half_ring = n_dev // 2
+    base_dev = me - core + half_ring
+    side_dev = base_dev + 4 * core - 2
+    far_copies = []
+    for smp in range(2):
+        far_copies.append(remote(lat.at[smp], z_far.at[1 + core], zf_send.at[smp], zf_recv.at[1 + core], lax.rem(base_dev + smp, n_dev)))
+        far_copies.append(remote(lat.at[smp], z_far.at[3 - 3 * core], zf_send.at[2 + smp], zf_recv.at[3 - 3 * core],
+                                 lax.rem(side_dev + smp, n_dev)))
+    for copy in far_copies:
+        copy.start()
     for copy in z_copies:
         copy.wait()
     rows = [jnp.where(me > 0, z_halo[0], 0.0)] + rows + [jnp.where(me < n_dev - 1, z_halo[1], 0.0)]
     lane = lax.broadcasted_iota(jnp.int32, (2 * n_z, width), 1)
-    for tap in range(9):
-        dy, dx = tap // 3, tap % 3
-        moved = rows[dy:dy + n_rows]
-        if dx == 0:
-            moved = [jnp.where(lane == 0, 0.0, pltpu.roll(row, 1, 1)) for row in moved]
-        if dx == 2:
-            moved = [jnp.where(lane == width - 1, 0.0, pltpu.roll(row, width - 1, 1)) for row in moved]
-        z_col[tap * 2 * n_z:(tap + 1) * 2 * n_z, :] = jnp.concatenate(moved, axis=1)
+
+    def columns(lines):
+        n_out = len(lines) - 2
+        for tap in range(9):
+            dy, dx = tap // 3, tap % 3
+            moved = lines[dy:dy + n_out]
+            if dx == 0:
+                moved = [jnp.where(lane == 0, 0.0, pltpu.roll(line, 1, 1)) for line in moved]
+            if dx == 2:
+                moved = [jnp.where(lane == width - 1, 0.0, pltpu.roll(line, width - 1, 1)) for line in moved]
+            z_col[tap * 2 * n_z:(tap + 1) * 2 * n_z, :n_out * width] = jnp.concatenate(moved, axis=1)
+        z_tok[:n_out * width, :] = jnp.transpose(z_col[:, :n_out * width]).astype(BF16)
+
     z_col[18 * n_z:, :] = jnp.zeros((128 - 18 * n_z, n_tok), F32)
-    z_tok[...] = jnp.transpose(z_col[...]).astype(BF16)
+    columns(rows)
 
     def first(smp, carry):
         total = jnp.dot(z_tok[...], w_first[smp], preferred_element_type=F32) + row_of(B_IN)
@@ -213,18 +251,20 @@
         return carry
 
     lax.fori_loop(0, 2, stage0, 0)
-    load_weights(2).start()
     load_weights(1).wait()
 
-    def forward(idx):
-        return remote(ring.at[idx], ring.at[idx + 2], rg_send.at[0, idx], rg_recv.at[idx + 2], ahead)
-
-    def backward(idx):
-        src = 1 - idx if isinstance(idx, int) and idx < 2 else idx + 7
+    def forward(src, idx):
+        slot = idx + 1 + idx // 5
+        return remote(ring.at[src], ring.at[slot], rg_send.at[0, idx], rg_recv.at[slot], ahead)
+
+    def backward(src, idx):
         return remote(ring.at[src], ring.at[idx + 9], rg_send.at[1, idx], rg_recv.at[idx + 9], behind)
 
+    def arrived(slot):
+        remote(ring.at[slot], ring.at[slot], rg_send.at[0, 0], rg_recv.at[slot], behind).wait_recv()
+
     def swap():
-        return remote(hbuf.at[1 - core], ring.at[1], sw_send, sw_recv, mate)
+        return remote(hbuf.at[1 - core], ring.at[8], sw_send, sw_recv, mate)
 
     def stage1(smp, carry):
         sums = conv_sample(smp, 1, 1, 1, 1, tbuf, hbuf, hbuf)
@@ -237,16 +277,15 @@
         @pl.when(smp == core)
         def _():
             ring[0] = hbuf[smp]
-            forward(0).start()
-            backward(1).start()
+            forward(0, 0).start()
+            backward(0, 1).start()
 
         return carry
 
     lax.fori_loop(0, 2, stage1, 0)
-    load_weights(3).start()
     swap().wait()
-    forward(1).start()
-    backward(0).start()
+    forward(8, 1).start()
+    backward(8, 0).start()
     load_att.wait()
     wabuf[1] = jnp.transpose(wabuf[1].astype(F32)).astype(BF16)
     bk_col[...] = jnp.transpose(jnp.broadcast_to(row_of(B_ATT + 1), (128, n_chan)))
@@ -255,21 +294,27 @@
     wait_stats(2, 1 - core)
     mul2, add2 = affine(2, core, 2)
     scale = n_chan ** -0.5 * math.log2(math.e)
-    mx[...] = jnp.full(mx.shape, -jnp.inf, F32)
-    ls[...] = jnp.zeros(ls.shape, F32)
-    acc[...] = jnp.zeros(acc.shape, F32)
+    q_len = n_tok // 2
+
+    def clear(blk, carry):
+        rows = pl.ds(blk * q_len, q_len)
+        mx[rows, :] = jnp.full((q_len, 128), -jnp.inf, F32)
+        ls[rows, :] = jnp.zeros((q_len, 128), F32)
+        acc[rows, :] = jnp.zeros((q_len, n_chan), F32)
+        return carry
+
+    lax.fori_loop(0, 4, clear, 0)
 
     def norm_slot(slot):
         nbuf[...] = (ring[slot].astype(F32) * mul2 + add2).astype(BF16)
 
     def query(slot, carry):
-        norm_slot(slot)
+        norm_slot(8 * slot)
         proj = jnp.dot(nbuf[...], wabuf[0], preferred_element_type=F32) + row_of(B_ATT)
         qbuf[pl.ds(slot * n_tok, n_tok), :] = proj.astype(BF16)
         return carry
 
     lax.fori_loop(0, 2, query, 0)
-    q_len = n_tok // 2
 
     def attend(slot):
         norm_slot(slot)
@@ -298,48 +343,117 @@
             acc[rows, :] = acc[rows, :] * fade[:, 0:1] + jnp.dot(prob, vbuf[...], preferred_element_type=F32)
             scores = following
 
-    def own(slot, carry):
-        attend(slot)
-        return carry
-
-    lax.fori_loop(0, 2, own, 0)
+    far = lax.rem(me - core + half_ring, n_dev)
+    far_rows = n_rows + 4
+
+    def far_first(part):
+        band = far + part
+        inside = (band > 0, band < n_dev - 1)
+
+        @pl.when(part == 0)
+        def _():
+            for slot in range(4):
+                remote(lat.at[0], z_far.at[slot], zf_send.at[slot], zf_recv.at[slot], mate).wait()
+
+        blank_z = jnp.zeros((n_z, width), F32)
+
+        def line(slot, row, keep):
+            val = z_far[slot, row].astype(F32)
+            if keep is not None:
+                val = jnp.where(keep, val, 0.0)
+            return jnp.concatenate([val, blank_z], axis=0)
+
+        lines = [line(part, n_rows - 3 + row, inside[0]) for row in range(3)]
+        lines += [line(part + 1, row, None) for row in range(n_rows)]
+        lines += [line(part + 2, row, inside[1]) for row in range(3)]
+        half_far = far_rows // 2
+        for idx in range(2):
+            columns(lines[idx * half_far:(idx + 1) * half_far + 2])
+            total = jnp.dot(z_tok[:half_far * width, :], w_first[0], preferred_element_type=F32) + row_of(B_IN)
+            far_in[idx * half_far * width:(idx + 1) * half_far * width, :] = total.astype(BF16)
+        mul, add = affine(0, core, 0)
+
+        def store(base, span, val):
+            far_mid[base:base + span, :] = val
+
+        conv_core(n_rows + 2, 2, lambda row: far_in[pl.ds(row * width, width), :], inside[0], inside[1], mul, add, 0, None, store)
+
+    def far_second(part):
+        band = far + part
+        mul, add = affine(1, core, 1)
+
+        def store(base, span, val):
+            ring[6 + 9 * part, base:base + span, :] = val
+
+        conv_core(n_rows, 1, lambda row: far_mid[pl.ds(row * width, width), :], band > 0, band < n_dev - 1, mul, add, 1,
+                  lambda base, span: far_in[base + 2 * width:base + 2 * width + span, :], store)
 
     def step(idx, carry):
-        forward(idx - 1).wait_recv()
-
-        @pl.when(idx <= 5)
-        def _():
-            forward(idx + 1).start()
-
-        remote(ring.at[idx + 8], ring.at[idx + 8], rg_send.at[1, idx - 1], rg_recv.at[idx + 8], behind).wait_recv()
-
-        @pl.when(idx <= 5)
-        def _():
-            backward(idx + 1).start()
-
-        def both(side, inner):
-            attend(idx + 1 + 7 * side)
-            return inner
-
-        return lax.fori_loop(0, 2, both, carry)
-
-    lax.fori_loop(1, 8, step, 0)
+        half = idx // 2
+        odd = idx % 2
+
+        @pl.when((idx == 2) | (idx == 6))
+        def _():
+            far_first(idx // 4)
+
+        @pl.when((idx == 4) | (idx == 8))
+        def _():
+            far_second(idx // 4 - 1)
+
+        @pl.when(idx == 8)
+        def _():
+            load_weights(2).start()
+            load_weights(3).start()
+
+        @pl.when((odd == 0) & (idx >= 2) & (idx != 12))
+        def _():
+            arrived(half)
+
+            @pl.when(idx <= 8)
+            def _():
+                forward(half, half + 1).start()
+
+        @pl.when((odd == 1) & (idx >= 3) & (idx <= 13))
+        def _():
+            arrived(8 + half)
+
+            @pl.when(idx <= 9)
+            def _():
+                backward(8 + half, half + 1).start()
+
+        attend(half + 8 * odd)
+        return carry
+
+    lax.fori_loop(0, n_dev, step, 0)
 
     def drain(idx, carry):
-        forward(idx).wait_send()
-        remote(ring.at[0], ring.at[9], rg_send.at[1, idx], rg_recv.at[9], behind).wait_send()
-        return carry
-
-    lax.fori_loop(0, 7, drain, 0)
-
-    def finish(base):
-        total = jnp.sum(ls[base:base + n_tok, :], axis=1, keepdims=True)
-        return (acc[base:base + n_tok, :] / total).astype(BF16)
-
-    vbuf[...] = finish(n_tok)
+        forward(0, idx).wait_send()
+        backward(0, idx).wait_send()
+        return carry
+
+    lax.fori_loop(0, 6, drain, 0)
+
+    def finish(base, put_out):
+        part = q_len // 2
+
+        def one(blk, carry):
+            rows = pl.ds(base + blk * part, part)
+            total = jnp.sum(ls[rows, :], axis=1, keepdims=True)
+            put_out(pl.ds(blk * part, part), (acc[rows, :] / total).astype(BF16))
+            return carry
+
+        lax.fori_loop(0, 4, one, 0)
+
+    def to_mate(rows, val):
+        vbuf[rows, :] = val
+
+    def to_self(rows, val):
+        obuf[0, rows, :] = val
+
+    finish(n_tok, to_mate)
     give = remote(vbuf, obuf.at[1], o_send, o_recv, mate)
     give.start()
-    obuf[0] = finish(0)
+    finish(0, to_self)
 
     def project(side, carry):
         @pl.when(side == 1)
@@ -390,7 +504,7 @@
     scratch = [
         vmem((2, n_tok, n_chan), BF16),
         vmem((2, n_tok, n_chan), BF16),
-        vmem((n_tok + 2 * width, 3 * n_chan), BF16),
+        vmem((n_tok + 4 * width, 3 * n_chan), BF16),
         vmem((2, 9 * n_chan, n_chan), BF16),
         vmem((4, n_chan, n_chan), BF16),
         vmem((4, 2, 2, width, n_chan), BF16),
@@ -412,8 +526,11 @@
         vmem((2, 2 * n_z, width), F32),
         vmem((128, n_tok), F32),
         vmem((n_tok, 128), BF16),
-        dma((2,)), dma, dma((5, 2)), dma((5, 2)), dma((4, 2, 2)), dma((4, 2, 2)), dma((2, 7)), dma((16,)),
-        dma, dma, dma, dma, dma((2,)), dma((2,)), dma((2,)),
+        vmem((4, n_rows, n_z, width), BF16),
+        vmem((n_tok + 4 * width, n_chan), BF16),
+        vmem((n_tok + 2 * width, n_chan), BF16),
+        dma((2,)), dma, dma((5, 2)), dma((5, 2)), dma((4, 2, 2)), dma((4, 2, 2)), dma((2, 6)), dma((n_dev,)),
+        dma, dma, dma, dma, dma((2,)), dma((2,)), dma((2,)), dma((4,)), dma((4,)),
     ]
     return pl.pallas_call(
         functools.partial(body, (n_dev, n_rows, width, n_chan)),
@@ -431,7 +548,7 @@
     def local_fn(latents, w_in, b_in, w_conv, b_conv, gn_scale, gn_shift, w_attn, b_attn):
         n_batch, n_rows, width, n_z = latents.shape
         n_chan = w_in.shape[-1]
-        out = decoder(n_dev, latents.transpose(0, 1, 3, 2), w_in.reshape(9, n_z, n_chan), b_in.reshape(1, n_chan), b_conv, gn_scale,
+        out = decoder(n_dev, latents.transpose(0, 1, 3, 2), w_in.reshape(9, n_z, n_chan), b_in, b_conv, gn_scale,
                       gn_shift, b_attn, w_conv.reshape(4, 9 * n_chan, n_chan), w_attn)
         return out.reshape(n_batch, n_rows, width, n_chan)
 

time: 259 us -> 247 us (0.954)
  Pallas kernels: 254 us -> 243 us
    pallas_call x1, Pallas kernels: 254 us -> 243 us  [decoder(): pl.pallas_call(functools.partial(body, (n_dev, n_rows, width, n_chan)), o...]
where the time goes in v3:
time: 247 us; the launch traced here: 246 us
  Pallas kernels  243 us (98%)
  local copies, waits for them, and re-layouts  3.1 us (1%)
    pallas_call x1, Pallas kernels, decoder(): pl.pallas_call(functools.partial(body, (n_dev, n_rows, width, n_chan)), o...  243 us

profile of v3, /device:TPU:21, one launch (start us, length us, event | category | flops | bytes accessed | tf_op | source)
XLA Modules:
  0.0 246.0 jit_solution(1137294323081394115)
XLA Ops:
  0.0 242.9 %shard_map.91 = bf16[2,1024,512]{2,1,0:T(8,128)(2,1)} custom-call(bf16[2,8,4,128]{3,2,1,0:T(4,128)(2,1)} %bitcast.7, bf16[9,4,512]{2,1,0:T(4,128)(2,1)} %bitcast.6, bf16[512]{0:T(512)(128)(2,1)} %b_in.1, bf16[4,512]{1,0:T(4,128)(2,1)} %b_conv.1, bf16[5,512]{1,0:T(8,128)(2,1)} %gain.1, bf16[5,512]{1,0:T(8,128)(2,1)} %shift.1, bf16[4,512]{1,0:T(4,128)(2,1)} %b_att.1, ...), custom_call_target="tpu_custom_call" | custom-call | tf_op jit(solution)/shard_map/pallas_call | solution.py:535
  242.9 3.1 %copy.11 = bf16[2,8,128,512]{3,2,1,0:T(8,128)(2,1)} copy(bf16[2,8,128,512]{3,2,1,0:T(8,128)(2,1)} %bitcast.5) | data formatting | bytes 4194304

commit v4 on v3

--- a/solution.py
+++ b/solution.py
@@ -13,7 +13,7 @@
 GROUPS = 32
 GN_EPS = 1e-6
 MESH = pl.DeviceIdType.MESH
-B_IN, B_CONV, GAIN, SHIFT, B_ATT, N_PAR = 0, 1, 5, 10, 15, 24
+B_IN, B_CONV, GAIN, SHIFT, B_ATT, NORM_ATT, N_PAR = 0, 1, 5, 10, 15, 19, 24
 
 
 def group_total(x_val, steps):
@@ -242,58 +242,9 @@
 
     lax.fori_loop(0, 2, first, 0)
 
-    load_weights(0).wait()
-
-    def stage0(smp, carry):
-        sums = conv_sample(smp, 0, 0, 0, 0, hbuf, tbuf, None)
-        send_halo(1, smp, tbuf)
-        send_stats(1, smp, sums)
-        return carry
-
-    lax.fori_loop(0, 2, stage0, 0)
-    load_weights(1).wait()
-
-    def forward(src, idx):
-        slot = idx + 1 + idx // 5
-        return remote(ring.at[src], ring.at[slot], rg_send.at[0, idx], rg_recv.at[slot], ahead)
-
-    def backward(src, idx):
-        return remote(ring.at[src], ring.at[idx + 9], rg_send.at[1, idx], rg_recv.at[idx + 9], behind)
-
-    def arrived(slot):
-        remote(ring.at[slot], ring.at[slot], rg_send.at[0, 0], rg_recv.at[slot], behind).wait_recv()
-
-    def swap():
-        return remote(hbuf.at[1 - core], ring.at[8], sw_send, sw_recv, mate)
-
-    def stage1(smp, carry):
-        sums = conv_sample(smp, 1, 1, 1, 1, tbuf, hbuf, hbuf)
-        send_stats(2, smp, sums)
-
-        @pl.when(smp == 1 - core)
-        def _():
-            swap().start()
-
-        @pl.when(smp == core)
-        def _():
-            ring[0] = hbuf[smp]
-            forward(0, 0).start()
-            backward(0, 1).start()
-
-        return carry
-
-    lax.fori_loop(0, 2, stage1, 0)
-    swap().wait()
-    forward(8, 1).start()
-    backward(8, 0).start()
     load_att.wait()
     wabuf[1] = jnp.transpose(wabuf[1].astype(F32)).astype(BF16)
     bk_col[...] = jnp.transpose(jnp.broadcast_to(row_of(B_ATT + 1), (128, n_chan)))
-
-    wait_stats(2, core)
-    wait_stats(2, 1 - core)
-    mul2, add2 = affine(2, core, 2)
-    scale = n_chan ** -0.5 * math.log2(math.e)
     q_len = n_tok // 2
 
     def clear(blk, carry):
@@ -305,8 +256,52 @@
 
     lax.fori_loop(0, 4, clear, 0)
 
+    load_weights(0).wait()
+
+    def stage0(smp, carry):
+        sums = conv_sample(smp, 0, 0, 0, 0, hbuf, tbuf, None)
+        send_halo(1, smp, tbuf)
+        send_stats(1, smp, sums)
+        return carry
+
+    lax.fori_loop(0, 2, stage0, 0)
+    load_weights(1).wait()
+
+    def forward(src, idx):
+        slot = idx + 1 + idx // 5
+        return remote(ring.at[src], ring.at[slot], rg_send.at[0, idx], rg_recv.at[slot], ahead)
+
+    def backward(src, idx):
+        slot = idx + 9 + idx // 5
+        return remote(ring.at[src], ring.at[slot], rg_send.at[1, idx], rg_recv.at[slot], behind)
+
+    def arrived(slot):
+        remote(ring.at[slot], ring.at[slot], rg_send.at[0, 0], rg_recv.at[slot], behind).wait_recv()
+
+    def swap():
+        return remote(hbuf.at[1 - core], ring.at[8], sw_send, sw_recv, mate)
+
+    def stage1(smp, carry):
+        sums = conv_sample(smp, 1, 1, 1, 1, tbuf, hbuf, hbuf)
+        send_stats(2, smp, sums)
+
+        @pl.when(smp == 1 - core)
+        def _():
+            swap().start()
+
+        @pl.when(smp == core)
+        def _():
+            ring[0] = hbuf[smp]
+            forward(0, 0).start()
+            backward(0, 1).start()
+
+        return carry
+
+    lax.fori_loop(0, 2, stage1, 0)
+    scale = n_chan ** -0.5 * math.log2(math.e)
+
     def norm_slot(slot):
-        nbuf[...] = (ring[slot].astype(F32) * mul2 + add2).astype(BF16)
+        nbuf[...] = (ring[slot].astype(F32) * row_of(NORM_ATT) + row_of(NORM_ATT + 1)).astype(BF16)
 
     def query(slot, carry):
         norm_slot(8 * slot)
@@ -314,12 +309,12 @@
         qbuf[pl.ds(slot * n_tok, n_tok), :] = proj.astype(BF16)
         return carry
 
-    lax.fori_loop(0, 2, query, 0)
 
     def attend(slot):
         norm_slot(slot)
         keys = lax.dot_general(wabuf[1], nbuf[...], (((1,), (1,)), ((), ())), preferred_element_type=F32)
         kt[...] = (keys + bk_col[:, 0:1]).astype(BF16)
+        scores = jnp.dot(qbuf[:q_len, :], kt[...], preferred_element_type=F32)
         vals = jnp.dot(nbuf[...], wabuf[2], preferred_element_type=F32) + row_of(B_ATT + 2)
         vbuf[...] = vals.astype(BF16)
 
@@ -328,7 +323,6 @@
 
         n_part = max(n_tok // 128, 1)
         wide = n_tok // n_part
-        scores = score(0)
         for blk in range(4):
             following = score(blk + 1) if blk < 3 else None
             rows = slice(blk * q_len, (blk + 1) * q_len)
@@ -340,7 +334,7 @@
             mx[rows, :] = new
             ls[rows, :wide] = ls[rows, :wide] * fade[:, :wide] + functools.reduce(jnp.add, prob)
             prob = jnp.concatenate([col.astype(BF16) for col in prob], axis=1)
-            acc[rows, :] = acc[rows, :] * fade[:, 0:1] + jnp.dot(prob, vbuf[...], preferred_element_type=F32)
+            acc[rows, :] = acc[rows, :] * jnp.concatenate([fade] * n_vreg, axis=1) + jnp.dot(prob, vbuf[...], preferred_element_type=F32)
             scores = following
 
     far = lax.rem(me - core + half_ring, n_dev)
@@ -383,7 +377,7 @@
         mul, add = affine(1, core, 1)
 
         def store(base, span, val):
-            ring[6 + 9 * part, base:base + span, :] = val
+            ring[6 + 8 * part, base:base + span, :] = val
 
         conv_core(n_rows, 1, lambda row: far_mid[pl.ds(row * width, width), :], band > 0, band < n_dev - 1, mul, add, 1,
                   lambda base, span: far_in[base + 2 * width:base + 2 * width + span, :], store)
@@ -392,32 +386,39 @@
         half = idx // 2
         odd = idx % 2
 
-        @pl.when((idx == 2) | (idx == 6))
+        @pl.when((idx == 0) | (idx == 4))
         def _():
             far_first(idx // 4)
 
-        @pl.when((idx == 4) | (idx == 8))
-        def _():
-            far_second(idx // 4 - 1)
+        @pl.when((idx == 2) | (idx == 8))
+        def _():
+            far_second(idx // 8)
 
         @pl.when(idx == 8)
         def _():
             load_weights(2).start()
             load_weights(3).start()
 
-        @pl.when((odd == 0) & (idx >= 2) & (idx != 12))
-        def _():
-            arrived(half)
-
-            @pl.when(idx <= 8)
+        @pl.when(idx == 0)
+        def _():
+            swap().wait()
+            forward(8, 1).start()
+            backward(8, 0).start()
+            wait_stats(2, core)
+            mul, add = affine(2, core, 2)
+            par[NORM_ATT:NORM_ATT + 1, :] = mul
+            par[NORM_ATT + 1:NORM_ATT + 2, :] = add
+            lax.fori_loop(0, 2, query, 0)
+
+        @pl.when((idx >= 2) & (half != 6))
+        def _():
+            arrived(half + 8 * odd)
+
+            @pl.when((half <= 4) & (odd == 0))
             def _():
                 forward(half, half + 1).start()
 
-        @pl.when((odd == 1) & (idx >= 3) & (idx <= 13))
-        def _():
-            arrived(8 + half)
-
-            @pl.when(idx <= 9)
+            @pl.when((half <= 4) & (odd == 1))
             def _():
                 backward(8 + half, half + 1).start()
 
@@ -432,6 +433,7 @@
         return carry
 
     lax.fori_loop(0, 6, drain, 0)
+    wait_stats(2, 1 - core)
 
     def finish(base, put_out):
         part = q_len // 2

time: 247 us -> 243 us (0.984)
  Pallas kernels: 243 us -> 240 us
    pallas_call x1, Pallas kernels: 243 us -> 240 us  [decoder(): pl.pallas_call(functools.partial(body, (n_dev, n_rows, width, n_chan)), o...]
where the time goes in v4:
time: 243 us
  Pallas kernels  240 us (99%)
  local copies, waits for them, and re-layouts  3.1 us (1%)
    pallas_call x1, Pallas kernels, decoder(): pl.pallas_call(functools.partial(body, (n_dev, n_rows, width, n_chan)), o...  240 us

profile of v4, /device:TPU:21, one launch (start us, length us, event | category | flops | bytes accessed | tf_op | source)
XLA Modules:
  0.0 243.2 jit_solution(3264072343086975432)
XLA Ops:
  0.0 240.1 %shard_map.91 = bf16[2,1024,512]{2,1,0:T(8,128)(2,1)} custom-call(bf16[2,8,4,128]{3,2,1,0:T(4,128)(2,1)} %bitcast.7, bf16[9,4,512]{2,1,0:T(4,128)(2,1)} %bitcast.6, bf16[512]{0:T(512)(128)(2,1)} %b_in.1, bf16[4,512]{1,0:T(4,128)(2,1)} %b_conv.1, bf16[5,512]{1,0:T(8,128)(2,1)} %gain.1, bf16[5,512]{1,0:T(8,128)(2,1)} %shift.1, bf16[4,512]{1,0:T(4,128)(2,1)} %b_att.1, ...), custom_call_target="tpu_custom_call" | custom-call | tf_op jit(solution)/shard_map/pallas_call | solution.py:537
  240.1 3.1 %copy.11 = bf16[2,8,128,512]{3,2,1,0:T(8,128)(2,1)} copy(bf16[2,8,128,512]{3,2,1,0:T(8,128)(2,1)} %bitcast.5) | data formatting | bytes 4194304

commit v5 on v4

--- a/solution.py
+++ b/solution.py
@@ -293,7 +293,7 @@
         def _():
             ring[0] = hbuf[smp]
             forward(0, 0).start()
-            backward(0, 1).start()
+            backward(0, 0).start()
 
         return carry
 
@@ -403,7 +403,7 @@
         def _():
             swap().wait()
             forward(8, 1).start()
-            backward(8, 0).start()
+            backward(8, 1).start()
             wait_stats(2, core)
             mul, add = affine(2, core, 2)
             par[NORM_ATT:NORM_ATT + 1, :] = mul

time: 243 us -> 243 us (level)
  no operation moved by 1% of the time
where the time goes in v5:
time: 243 us
  Pallas kernels  240 us (99%)
  local copies, waits for them, and re-layouts  3.1 us (1%)
    pallas_call x1, Pallas kernels, decoder(): pl.pallas_call(functools.partial(body, (n_dev, n_rows, width, n_chan)), o...  240 us

profile of v5, /device:TPU:21, one launch (start us, length us, event | category | flops | bytes accessed | tf_op | source)
XLA Modules:
  0.0 243.2 jit_solution(18351981450916477867)
XLA Ops:
  0.0 240.1 %shard_map.91 = bf16[2,1024,512]{2,1,0:T(8,128)(2,1)} custom-call(bf16[2,8,4,128]{3,2,1,0:T(4,128)(2,1)} %bitcast.7, bf16[9,4,512]{2,1,0:T(4,128)(2,1)} %bitcast.6, bf16[512]{0:T(512)(128)(2,1)} %b_in.1, bf16[4,512]{1,0:T(4,128)(2,1)} %b_conv.1, bf16[5,512]{1,0:T(8,128)(2,1)} %gain.1, bf16[5,512]{1,0:T(8,128)(2,1)} %shift.1, bf16[4,512]{1,0:T(4,128)(2,1)} %b_att.1, ...), custom_call_target="tpu_custom_call" | custom-call | tf_op jit(solution)/shard_map/pallas_call | solution.py:537
  240.1 3.1 %copy.11 = bf16[2,8,128,512]{3,2,1,0:T(8,128)(2,1)} copy(bf16[2,8,128,512]{3,2,1,0:T(8,128)(2,1)} %bitcast.5) | data formatting | bytes 4194304
